TPU v7x, 32 devices: a whole 2x2x4 slice. The times are simulated.
32 devices in a mesh: seq: 8 (over z, x), vocab: 4 (over y, core).
Axes of the slice: x: 2, y: 2, z: 4, core: 2. Of those that a mesh axis runs over, the one named last changes fastest.
Arguments:
- hidden: bfloat16 [2, 1024, 2048], P(None, 'seq'), may hold values from -6 to 6
- embedded: bfloat16 [2, 1024, 2048], P(None, 'seq'), may hold values from -6 to 6
- targets: int32 [2, 1024], P(None, 'seq'), may hold values from 0 to 51199
- main_mask: int32 [2, 1024], P(None, 'seq'), may hold values 0 or 1
- mtp_mask: int32 [2, 1024], P(None, 'seq'), may hold values from 0 to 1, as said below
- lengths: int32 [2], replicated, may hold values from 256 to 1024, as said below
- head_weight: bfloat16 [2048, 51200], P(None, ('seq', 'vocab')), may hold values from -7.6733202 to 7.6733202
- projection: bfloat16 [4096, 2048], P(None, 'vocab'), may hold values from -0.09375 to 0.09375
- main_gain: float32 [2048], replicated, may hold values from 0.5 to 1.5
- hidden_gain: float32 [2048], replicated, may hold values from 0.5 to 1.5
- embed_gain: float32 [2048], replicated, may hold values from 0.5 to 1.5
- mtp_gain: float32 [2048], replicated, may hold values from 0.5 to 1.5
Outputs:
- main_tokens: float32 [2, 1024], P(None, 'seq')
- mtp_tokens: float32 [2, 1024], P(None, 'seq')
- total_loss: float32 [], replicated
Inputs may be any that keep to these rules, and one draw needn't show every extreme that they name: `mtp_mask`: 1 at every position that is a multiple of 128. `lengths`: the first sequence has length 1024.
All inputs are finite; a program needn't handle non-finite values. No bound on the sum of `main_mask` on one device may be relied on, other than what follows from the above.
Results may differ from a plain program's by a relative error of at most 0.0004.
The roundings to bfloat16 on the way count: a program that leaves them out, or rounds other values in their place, can miss the bound.
Values may be sent and summed in bfloat16 or wider, within the bound.
No kernel may reach another device: no remote copies, remote signals or barrier semaphores. Data moves between devices by JAX's collectives and lax.ppermute only.
A program may use at most 128 MiB of HBM per device.

v0:
```python
import jax
import jax.numpy as jnp
from jax import lax
from jax.sharding import PartitionSpec as P

EPSILON = 1e-06
MTP_WEIGHT = 0.3


def from_behind(block, axis, distance):
    devices = range(lax.axis_size(axis))
    route = [(i - distance, i) for i in devices if i - distance in devices]
    return lax.ppermute(block, axis, route)


def partner_2(value, axis, apart):
    mask = 2**apart
    pairs = [(source, source ^ mask) for source in range(lax.axis_size(axis))]
    return lax.ppermute(value, axis, pairs)


def normalize(values, gain_vec):
    values = values.astype(jnp.float32)
    mean_square = jnp.mean(values * values, axis=-1, keepdims=True)
    return values * lax.rsqrt(mean_square + EPSILON) * gain_vec


def column_stats(logits, column_ids, wanted):
    highest = jnp.max(logits, axis=1)
    exp_total = jnp.sum(jnp.exp(logits - highest[:, None]), axis=1)
    picked = jnp.sum(jnp.where(column_ids[None, :] == wanted[:, None], logits, 0.0), axis=1)
    return (highest, exp_total, picked)


def join_stats(earlier, latter):
    highest = jnp.maximum(earlier[0], latter[0])
    exp_total = earlier[1] * jnp.exp(earlier[0] - highest) + latter[1] * jnp.exp(
        latter[0] - highest
    )
    return (highest, exp_total, earlier[2] + latter[2])


def shards(
    hidden,
    embedded,
    targets,
    main_mask,
    mtp_mask,
    lengths,
    head_weight,
    projection,
    main_gain,
    hidden_gain,
    embed_gain,
    mtp_gain,
):
    batches, seq_len, model_width = hidden.shape
    seq_index = lax.axis_index("seq")
    vocab_index = lax.axis_index("vocab")
    vocab_count = lax.axis_size("vocab")
    block_cols = head_weight.shape[1]
    positions = seq_index * seq_len + lax.broadcasted_iota(jnp.int32, (batches, seq_len), 1)
    length_col = lengths[:, None]
    keep_main = ((main_mask == 1) & (positions + 1 < length_col)).astype(jnp.float32)
    keep_mtp = ((mtp_mask == 1) & (positions >= 1) & (positions + 1 < length_col)).astype(
        jnp.float32
    )
    count_main = jnp.sum(keep_main)
    count_mtp = jnp.sum(keep_mtp)
    counted = lax.psum((count_main, count_mtp), "seq")
    main_rows = normalize(hidden, main_gain).astype(jnp.bfloat16).reshape(-1, model_width)
    incoming = from_behind(hidden[:, seq_len - 1 :, :], "seq", 1)
    previous = jnp.concatenate([incoming, hidden[:, : seq_len - 1, :]], axis=1)
    joined = jnp.concatenate(
        [normalize(previous, hidden_gain), normalize(embedded, embed_gain)], axis=2
    )
    joined = joined.astype(jnp.bfloat16).reshape(-1, 2 * model_width)
    partial_value = jnp.dot(joined, projection, preferred_element_type=jnp.float32).astype(
        jnp.bfloat16
    )
    mixed = lax.all_gather(partial_value, "vocab", axis=1, tiled=True)
    mtp_rows = normalize(mixed, mtp_gain).astype(jnp.bfloat16)
    all_rows = jnp.concatenate([main_rows, mtp_rows], axis=0)
    flat_targets = targets.reshape(-1)
    wanted = jnp.concatenate([flat_targets, flat_targets], axis=0)
    held_cols = head_weight
    levels = lax.axis_size("seq").bit_length() - 1
    for bit_number in range(1, levels):
        received = partner_2(held_cols, "seq", bit_number)
        upper_half = seq_index >> bit_number & 1 == 1
        held_cols = jnp.where(
            upper_half,
            jnp.concatenate([received, held_cols], axis=1),
            jnp.concatenate([held_cols, received], axis=1),
        )
    partner = partner_2(all_rows, "seq", 0)
    partner_wanted = partner_2(wanted, "seq", 0)
    column_pos = lax.broadcasted_iota(jnp.int32, (held_cols.shape[1],), 0)
    anchor_seq = (seq_index & 1) + 2 * (column_pos // block_cols)
    column_ids = (anchor_seq * vocab_count + vocab_index) * block_cols + column_pos % block_cols
    logits = jnp.dot(
        jnp.concatenate([all_rows, partner], axis=0), held_cols, preferred_element_type=jnp.float32
    )
    row_count = all_rows.shape[0]
    own_stats = column_stats(logits[:row_count], column_ids, wanted)
    peer_stats = column_stats(logits[row_count:], column_ids, partner_wanted)
    returned = partner_2((peer_stats[0], peer_stats[1], peer_stats[2]), "seq", 0)
    highest, exp_total, picked = join_stats(own_stats, returned)
    global_max = lax.pmax(highest, "vocab")
    global_total, target_logit = lax.psum(
        (exp_total * jnp.exp(highest - global_max), picked), "vocab"
    )
    losses = global_max + jnp.log(global_total) - target_logit
    half_rows = batches * seq_len
    main_tokens = keep_main * losses[:half_rows].reshape(batches, seq_len)
    mtp_tokens = keep_mtp * losses[half_rows:].reshape(batches, seq_len)
    main_sum = jnp.sum(main_tokens)
    mtp_sum = jnp.sum(mtp_tokens)
    summed = lax.psum((main_sum, mtp_sum), "seq")
    total_main, total_mtp = summed
    kept_main, kept_mtp = counted
    total_loss = total_main / jnp.maximum(kept_main, 1.0) + MTP_WEIGHT * total_mtp / jnp.maximum(
        kept_mtp, 1.0
    )
    return (main_tokens, mtp_tokens, total_loss)


def solution(mesh):
    return jax.shard_map(
        shards,
        mesh=mesh,
        in_specs=(
            P(None, "seq", None),
            P(None, "seq", None),
            P(None, "seq"),
            P(None, "seq"),
            P(None, "seq"),
            P(),
            P(None, ("seq", "vocab")),
            P(None, "vocab"),
            P(),
            P(),
            P(),
            P(),
        ),
        out_specs=(P(None, "seq"), P(None, "seq"), P()),
        check_vma=False,
    )
```

profile of v0, /device:TPU:0, one launch (start us, length us, event | category | flops | bytes accessed | tf_op | source)
XLA Modules:
  0.0 926.5 jit_solution(852602479931637078)
XLA Ops:
  7.2 0.0 all-gather.2.cloned.1.call-start
  7.2 3.1 collective-permute-start.2
  10.3 0.0 copy-start.1
  10.3 0.0 copy-start.2
  10.3 0.0 copy-start.3
  10.3 141.4 %collective-permute-done.2 = bf16[2048,1600]{0,1:T(8,128)(2,1)} collective-permute-done((bf16[2048,1600]{0,1:T(8,128)(2,1)}, bf16[2048,1600]{0,1:T(8,128)(2,1)}, u32[]{:S(2)}, u32[]{:S(2)}) %collective-permute-start.2) | collective-permute-done | bytes 6553632 | tf_op jit(solution)/shard_map/ppermute | solution.py:19
  151.8 15.6 %maximum_select_fusion.2 = bf16[2048,3200]{0,1:T(8,128)(2,1)} fusion(bf16[2048,1600]{0,1:T(8,128)(2,1)} %param.18, bf16[2048,1600]{0,1:T(8,128)(2,1)} %collective-permute-done.2, pred[]{:T(512)S(6)} %eq.40), kind=kLoop, calls=%fused_computation.8 | loop fusion | flops 58982400 | bytes 26214400 | tf_op jit(solution)/shard_map/jit(_where)/select_n | solution.py:91
  167.4 0.0 copy-start.4
  167.4 0.0 copy-start.11
  167.4 2.8 collective-permute-start.3
  170.2 0.0 copy-done.1
  170.2 3.4 collective-permute-start
  173.7 0.0 copy-done.2
  173.7 0.3 fusion.15
  174.0 0.0 copy-done.3
  174.0 0.3 fusion.17
  174.3 0.8 collective-permute-done
  175.1 0.4 multiply_reduce_fusion
  175.5 0.3 maximum_convert_fusion
  175.8 0.0 copy-done.4
  175.9 0.0 copy-start.5
  175.9 0.2 fusion.26
  176.1 0.0 copy-done.11
  176.1 0.0 copy-start.6
  176.1 2.0 fusion.27
  178.1 0.0 copy-start.7
  178.1 0.0 all-gather.2.cloned.1.call-update
  178.1 0.3 fusion.12
  178.4 0.0 copy-done.5
  178.4 0.3 fusion.14
  178.8 573.8 %all-gather.2.cloned.1.call-done = bf16[256,2048]{1,0:T(8,128)(2,1)} async-done(((bf16[256,512]{1,0:T(8,128)(2,1)}), bf16[256,2048]{1,0:T(8,128)(2,1)}) %all-gather.2.cloned.1.call-update) | async-done | bytes 1048592 | tf_op jit(solution)/shard_map/all_gather | solution.py:81
  752.6 1.5 fusion.18
  754.1 0.0 copy-done.6
  754.1 1.5 fusion.20
  755.6 1.5 pad_maximum_fusion
  757.1 1.5 collective-permute-start.1
  758.6 0.0 copy-done.7
  758.6 0.6 collective-permute-start.6
  759.3 45.9 %collective-permute-done.1 = bf16[512,2048]{1,0:T(8,128)(2,1)} collective-permute-done((bf16[512,2048]{1,0:T(8,128)(2,1)}, bf16[512,2048]{1,0:T(8,128)(2,1)}, u32[]{:S(2)}, u32[]{:S(2)}) %collective-permute-start.1) | collective-permute-done | bytes 2097184 | tf_op jit(solution)/shard_map/ppermute | solution.py:19
  805.2 0.0 collective-permute-done.3
  805.2 49.2 %fusion = f32[1024,6400]{1,0:T(8,128)} fusion(bf16[2048,3200]{0,1:T(8,128)(2,1)} %maximum_select_fusion.2, bf16[2048,3200]{0,1:T(8,128)(2,1)} %collective-permute-done.3, pred[]{:T(512)S(6)} %eq.39, bf16[512,2048]{1,0:T(8,128)(2,1)} %collective-permute-done.1, bf16[256,2048]{1,0:T(8,128)(2,1)S(1)} %fusion.20, bf16[256,2048]{1,0:T(8,128)(2,1)S(1)} %bitcast.22), kind=kOutput, calls=%fused_computation.1 | convolution fusion | flops 26974093312 | bytes 56623104 | tf_op jit(solution)/shard_map/dot_general | solution.py:101
  854.4 0.0 copy-start
  854.4 9.4 %slice_reduce_fusion = (f32[512]{0:T(512)S(1)}, f32[512]{0:T(512)S(1)}) fusion(f32[1024,6400]{1,0:T(8,128)} %fusion), kind=kLoop, calls=%fused_computation.13 | loop fusion | flops 6552576 | bytes 26218496 | tf_op jit(solution)/shard_map/reduce_max | solution.py:29
  863.8 1.5 collective-permute-start.4
  865.4 0.0 collective-permute-done.6
  865.4 5.0 copy-done
  870.4 0.0 copy-start.8
  870.4 0.0 copy-start.9
  870.4 0.0 copy-start.10
  870.4 6.9 exponential_reduce_fusion.1
  877.3 1.5 collective-permute-start.7
  878.8 0.0 copy-done.8
  878.9 0.0 copy-done.9
  878.9 0.0 copy-done.10
  878.9 0.8 convert_reduce_fusion
  879.6 0.6 collective-permute-start.5
  880.2 0.0 collective-permute-done.4
  880.2 0.8 collective-permute-done.7
  881.0 5.7 pmax.7
  886.7 0.0 collective-permute-done.5
  886.7 5.8 all-reduce.1
  892.5 1.2 fusion.47
  893.7 22.3 %all-reduce = (f32[]{:T(128)}, f32[]{:T(128)}, f32[]{:T(128)}, f32[]{:T(128)}) all-reduce(f32[]{:T(128)} %get-tuple-element.25, f32[]{:T(128)} %get-tuple-element.27, f32[]{:T(128)} %get-tuple-element.19, f32[]{:T(128)} %get-tuple-element.17), channel_id=1, replica_groups=mesh['seq'=8,'vocab'=4] {'seq'}, use_global_device_ids=true, to_apply=%region_14.15 | all-reduce | flops 4 | bytes 32 | tf_op jit(solution)/shard_map/psum | solution.py:119
  (13 shorter events, 0.1 us)
Async XLA Ops:
  7.2 745.4 %all-gather.2.cloned.1.call-start = ((), (), s32[]{:S(2)}) async-start(), calls=%async_computation | async-start | bytes 1310720 | tf_op jit(solution)/shard_map/all_gather | solution.py:81
  7.2 144.6 %collective-permute-start.2 = (bf16[2048,1600]{0,1:T(8,128)(2,1)}, bf16[2048,1600]{0,1:T(8,128)(2,1)}, u32[]{:S(2)}, u32[]{:S(2)}) collective-permute-start(bf16[2048,1600]{0,1:T(8,128)(2,1)} %param.18), channel_id=1, source_target_pairs={{0,8},{4,12},{8,0},{12,4},{16,24},{20,28},{24,16},{28,20},{1,9},{5... | collective-permute-start | bytes 19660808 | tf_op jit(solution)/shard_map/ppermute | solution.py:19
  10.3 159.9 %copy-start.1 = (bf16[2,128,2048]{2,1,0:T(8,128)(2,1)S(1)}, bf16[2,128,2048]{2,1,0:T(8,128)(2,1)}, u32[]{:S(2)}) copy-start(bf16[2,128,2048]{2,1,0:T(8,128)(2,1)} %param.12) | copy-start | bytes 3145732
  10.3 163.3 %copy-start.2 = (bf16[2,128,2048]{2,1,0:T(8,128)(2,1)S(1)}, bf16[2,128,2048]{2,1,0:T(8,128)(2,1)}, u32[]{:S(2)}) copy-start(bf16[2,128,2048]{2,1,0:T(8,128)(2,1)} %param.13) | copy-start | bytes 3145732
  10.3 163.6 %copy-start.3 = (f32[2048]{0:T(1024)S(1)}, f32[2048]{0:T(1024)}, u32[]{:S(2)}) copy-start(f32[2048]{0:T(1024)} %param.22) | copy-start | bytes 24580
  167.4 8.4 copy-start.4
  167.4 8.7 copy-start.11
  167.4 637.8 %collective-permute-start.3 = (bf16[2048,3200]{0,1:T(8,128)(2,1)}, bf16[2048,3200]{0,1:T(8,128)(2,1)}, u32[]{:S(2)}, u32[]{:S(2)}) collective-permute-start(bf16[2048,3200]{0,1:T(8,128)(2,1)} %maximum_select_fusion.2), channel_id=1, source_target_pairs={{0,16},{4,20},{8,24},{12,28},{16,0},{20,4},{24,8},{28,12},{1,17},{... | collective-permute-start | bytes 39321608 | tf_op jit(solution)/shard_map/ppermute | solution.py:19
  170.2 4.8 collective-permute-start
  175.9 2.6 copy-start.5
  176.1 578.0 %copy-start.6 = (f32[2048]{0:T(1024)S(1)}, f32[2048]{0:T(1024)}, u32[]{:S(2)}) copy-start(f32[2048]{0:T(1024)} %param.23) | copy-start | bytes 24580
  178.1 580.5 %copy-start.7 = (s32[2,128]{1,0:T(2,128)S(1)}, s32[2,128]{1,0:T(2,128)}, u32[]{:S(2)}) copy-start(s32[2,128]{1,0:T(2,128)} %param.14) | copy-start | bytes 3076
  757.1 48.1 %collective-permute-start.1 = (bf16[512,2048]{1,0:T(8,128)(2,1)}, bf16[512,2048]{1,0:T(8,128)(2,1)}, u32[]{:S(2)}, u32[]{:S(2)}) collective-permute-start(bf16[512,2048]{1,0:T(8,128)(2,1)} %pad_maximum_fusion), channel_id=1, source_target_pairs={{0,4},{4,0},{8,12},{12,8},{16,20},{20,16},{24,28},{28,24},{1,5},{5... | collective-permute-start | bytes 6291464 | tf_op jit(solution)/shard_map/ppermute | solution.py:19
  758.6 106.7 %collective-permute-start.6 = (s32[512]{0:T(512)S(1)}, s32[512]{0:T(512)S(1)}, u32[]{:S(2)}, u32[]{:S(2)}) collective-permute-start(s32[512]{0:T(512)S(1)} %pad_add_fusion), channel_id=1, source_target_pairs={{0,4},{4,0},{8,12},{12,8},{16,20},{20,16},{24,28},{28,24},{1,5},{5... | collective-permute-start | bytes 6152 | tf_op jit(solution)/shard_map/ppermute | solution.py:19
  854.4 16.0 %copy-start = (f32[1024,6400]{1,0:T(8,128)S(1)}, f32[1024,6400]{1,0:T(8,128)}, u32[]{:S(2)}) copy-start(f32[1024,6400]{1,0:T(8,128)} %fusion) | copy-start | bytes 78643200
  863.8 16.3 %collective-permute-start.4 = (f32[512]{0:T(512)S(1)}, f32[512]{0:T(512)S(1)}, u32[]{:S(2)}, u32[]{:S(2)}) collective-permute-start(f32[512]{0:T(512)S(1)} %get-tuple-element.9), channel_id=1, source_target_pairs={{0,4},{4,0},{8,12},{12,8},{16,20},{20,16},{24,28},{28,24},{1,5},{5... | collective-permute-start | bytes 6152 | tf_op jit(solution)/shard_map/ppermute | solution.py:19
  870.4 8.4 copy-start.8
  870.4 8.4 copy-start.9
  870.4 8.4 copy-start.10
  877.3 3.6 collective-permute-start.7
  879.6 7.1 collective-permute-start.5
Sparse Core Ops, SparseCore 0:
  178.3 574.2 all-gather.1
where the time goes:
time: 927 us; the launch traced here: 926 us
  waiting for transfers between devices  763 us (82%)
  matrix products  51.1 us (6%)
  other arithmetic  40.7 us (4%)
  blocking collectives  33.8 us (4%)
  between operations  17.9 us (2%)
  starting transfers between devices  15.1 us (2%)
    all_gather x1, waiting for transfers between devices, shards(): mixed = lax.all_gather(partial_value, 'vocab', axis=1, tiled=True)  574 us
    ppermute x7, waiting for transfers between devices, partner_2(): return lax.ppermute(value, axis, pairs)  188 us
    dot_general x1, matrix products, shards(): jnp.dot(jnp.concatenate([all_rows, partner], axis=0), held_cols, preferre...  49.2 us
    psum x1, blocking collectives, shards(): summed = lax.psum((main_sum, mtp_sum), 'seq')  22.3 us
  transfers between devices with their start and end apart: 9, of which 5 were waited for; matrix products, arithmetic and copies ran while one was open for 8% of the time, Pallas kernels for 0%

commit v1 on v0

v1 whole, which is shorter than its diff:
```python
import functools

import jax
import jax.numpy as jnp
from jax import lax
from jax.experimental import pallas as pl
from jax.experimental.pallas import tpu as pltpu
from jax.sharding import PartitionSpec as P

EPSILON = 1e-06
MTP_WEIGHT = 0.3
LOWEST = -1e30
NOWHERE = -(1 << 30)
META_ROWS = 8
ROW_ALIGN = 16
TILE_MAX = 800
AXES = ("seq", "vocab")


def normalize(values, gain_vec):
    values = values.astype(jnp.float32)
    mean_square = jnp.mean(values * values, axis=-1, keepdims=True)
    return values * lax.rsqrt(mean_square + EPSILON) * gain_vec


def column_tile(cols):
    return max(
        t for t in range(ROW_ALIGN, min(cols, TILE_MAX) + 1, ROW_ALIGN) if cols % t == 0
    )


def ring_order(mesh):
    count = mesh.shape["seq"]
    coords = [getattr(d, "coords", None) for d in mesh.devices[:, 0]]
    across = len({c[0] for c in coords}) if all(c is not None for c in coords) else 2
    if count % across or across < 2 or (count // across) % 2:
        return list(range(count))
    deep = count // across
    walk = [(0, x) for x in range(across)]
    for z in range(1, deep):
        line = list(range(1, across))
        walk += [(z, x) for x in (line[::-1] if z % 2 else line)]
    walk += [(z, 0) for z in range(deep - 1, 0, -1)]
    return [z * across + x for z, x in walk]


def head_kernel(blocks, valid, tile, count, *refs):
    scalars, stats_in, info_in, own, peer = refs[:5]
    sources = refs[5 : 5 + count]
    stats, info, x, wanted, top, total, picked, first, second = refs[5 + count :]
    span = x.shape[0] // len(blocks)
    cols = own.shape[0]
    steps = cols // tile
    stats[...] = stats_in[...]
    info[...] = info_in[...]
    half = stats.shape[1] // 2
    y = scalars[2]
    for at, (head, parts) in enumerate(blocks):
        slot = scalars[3 + at]
        for ref, start, rows, place in parts:
            shift = (0, y * rows, (1 - y) * rows)[place]
            to = pl.multiple_of(at * span + shift, rows)
            x[pl.ds(to, rows), :] = sources[ref][start : start + rows, :]
        if head == 0:
            meta = sources[parts[0][0]][span : span + META_ROWS, :span].astype(jnp.float32)
            ids = meta[0:1] * 256.0 + meta[1:2]
            info[0, pl.ds(slot, 1), :] = ids
            info[0, pl.ds(half + slot, 1), :] = ids
            info[1, pl.ds(slot, 1), :] = meta[2:3]
            info[1, pl.ds(half + slot, 1), :] = meta[3:4]
        ids = info[0, pl.ds(head * half + slot, 1), :].astype(jnp.int32)
        wanted[:, at * span : (at + 1) * span] = jnp.broadcast_to(ids, (8, span))
    top[...] = jnp.full(top.shape, LOWEST, jnp.float32)
    total[...] = jnp.zeros(total.shape, jnp.float32)
    picked[...] = jnp.zeros(picked.shape, jnp.float32)
    second[...] = jnp.full(second.shape, LOWEST, jnp.float32)

    def fold(held, start, base):
        logits = held[...].reshape(tile // 8, 8, x.shape[0])
        place = lax.broadcasted_iota(jnp.int32, logits.shape, 0) * 8
        place += lax.broadcasted_iota(jnp.int32, logits.shape, 1)
        if valid < cols:
            logits = jnp.where(place + start < valid, logits, LOWEST)
        old = top[...]
        new = jnp.maximum(old, jnp.max(logits, axis=0))
        top[...] = new
        fresh = jnp.sum(jnp.exp(logits - new[None]), axis=0)
        total[...] = total[...] * jnp.exp(old - new) + fresh
        hit = place == (wanted[...] - (base + start))[None]
        picked[...] += jnp.sum(jnp.where(hit, logits, 0.0), axis=0)

    def product(weights, start):
        return lax.dot_general(
            weights[pl.ds(start, tile), :],
            x[...],
            (((1,), (1,)), ((), ())),
            preferred_element_type=jnp.float32,
        )

    def step(j, _):
        start = pl.multiple_of(j * tile, tile)
        first[...] = product(own, start)
        fold(second, start - tile, jnp.where(j > 0, scalars[1], NOWHERE))
        second[...] = product(peer, start)
        fold(first, start, scalars[0])
        return 0

    lax.fori_loop(0, steps, step, 0)
    fold(second, cols - tile, scalars[1])
    highest = jnp.max(top[...], axis=0, keepdims=True)
    sums = jnp.sum(total[...] * jnp.exp(top[...] - highest), axis=0, keepdims=True)
    chosen = jnp.sum(picked[...], axis=0, keepdims=True)
    for at, (head, _) in enumerate(blocks):
        lanes = slice(at * span, (at + 1) * span)
        slot = pl.ds(head * half + scalars[3 + at], 1)
        stats[0, slot, :] = highest[:, lanes]
        stats[1, slot, :] = sums[:, lanes]
        stats[2, slot, :] = chosen[:, lanes]


def head_stats(scalars, state, own, peer, valid, sources, blocks):
    cols, width = own.shape
    tile = column_tile(cols)
    span = state[0].shape[2]
    rows = len(blocks) * span
    vmem = pl.BlockSpec(memory_space=pltpu.VMEM)
    wide = pltpu.VMEM((8, rows), jnp.float32)
    return pl.pallas_call(
        functools.partial(head_kernel, blocks, valid, tile, len(sources)),
        in_specs=[pl.BlockSpec(memory_space=pltpu.SMEM)] + [vmem] * (4 + len(sources)),
        out_specs=[vmem, vmem],
        out_shape=[jax.ShapeDtypeStruct(s.shape, s.dtype) for s in state],
        scratch_shapes=[
            pltpu.VMEM((rows, width), jnp.bfloat16),
            pltpu.VMEM((8, rows), jnp.int32),
            wide,
            wide,
            wide,
            pltpu.VMEM((tile, rows), jnp.float32),
            pltpu.VMEM((tile, rows), jnp.float32),
        ],
        compiler_params=pltpu.CompilerParams(vmem_limit_bytes=12 * 1024 * 1024),
        cost_estimate=pl.CostEstimate(
            flops=4 * rows * cols * width,
            bytes_accessed=4 * cols * width + 2 * rows * width,
            transcendentals=2 * rows * cols,
        ),
        name=f"head_{rows}",
    )(scalars, *state, own, peer, *sources)


def join_stats(earlier, latter):
    highest = jnp.maximum(earlier[0], latter[0])
    exp_total = earlier[1] * jnp.exp(earlier[0] - highest)
    exp_total += latter[1] * jnp.exp(latter[0] - highest)
    return jnp.stack([highest, exp_total, earlier[2] + latter[2]])


def ordered(swap, mine, other):
    return jnp.where(swap, other, mine), jnp.where(swap, mine, other)


def shards(
    order,
    hidden,
    embedded,
    targets,
    main_mask,
    mtp_mask,
    lengths,
    head_weight,
    projection,
    main_gain,
    hidden_gain,
    embed_gain,
    mtp_gain,
):
    batches, seq_len, model_width = hidden.shape
    seq_index = lax.axis_index("seq")
    vocab_index = lax.axis_index("vocab")
    seq_count = lax.axis_size("seq")
    vocab_count = lax.axis_size("vocab")
    core = vocab_index & 1
    row = vocab_index >> 1
    block_cols = head_weight.shape[1]
    span = batches * seq_len // 2

    def across(value, mask):
        pairs = [(v, v ^ mask) for v in range(vocab_count)]
        return lax.ppermute(value, "vocab", pairs)

    own = head_weight.T
    padding = -block_cols % ROW_ALIGN
    if padding:
        own = jnp.pad(own, ((0, padding), (0, 0)))
    peer = across(own, 1)

    route = [(i - 1, i) for i in range(1, seq_count)]
    incoming = lax.ppermute(hidden[:, seq_len - 1 :, :], "seq", route)

    positions = seq_index * seq_len + lax.broadcasted_iota(jnp.int32, (batches, seq_len), 1)
    inside = positions + 1 < lengths[:, None]
    keep_main = (main_mask == 1) & inside
    keep_mtp = (mtp_mask == 1) & inside & (positions >= 1)
    fields = jnp.stack(
        [targets // 256, targets % 256, keep_main.astype(jnp.int32), keep_mtp.astype(jnp.int32)]
    )

    def half(value):
        parts = value.reshape((2, span) + value.shape[1:])
        return parts

    flat_hidden = half(hidden.reshape(-1, model_width))
    mine = jnp.where(core == 0, flat_hidden[0], flat_hidden[1])
    main_rows = normalize(mine, main_gain).astype(jnp.bfloat16)
    flat_fields = fields.reshape(4, 2, span)
    meta = jnp.where(core == 0, flat_fields[:, 0], flat_fields[:, 1]).astype(jnp.bfloat16)
    meta = jnp.pad(meta, ((0, META_ROWS - 4), (0, model_width - span)))
    main_block = jnp.concatenate([main_rows, meta], axis=0)

    def flat(s, v):
        return s * vocab_count + v

    following = {s: order[(i + 1) % seq_count] for i, s in enumerate(order)}
    leading = {b: a for a, b in following.items()}
    onward = [
        (flat(s, v), flat((leading if v & 1 else following)[s], v))
        for s in range(seq_count)
        for v in range(vocab_count)
    ]
    backward = [(b, a) for a, b in onward]

    def hops(block, pairs, steps):
        found = []
        for _ in range(steps):
            block = lax.ppermute(block, AXES, pairs)
            found.append(block)
        return found

    far = seq_count // 2
    main_on = hops(main_block, onward, far)
    main_back = hops(main_block, backward, far - 1)

    previous = jnp.concatenate([incoming, hidden[:, : seq_len - 1, :]], axis=1)
    joined = jnp.concatenate(
        [normalize(previous, hidden_gain), normalize(embedded, embed_gain)], axis=2
    )
    joined = joined.astype(jnp.bfloat16).reshape(-1, 2 * model_width)
    partial_value = jnp.dot(joined, projection, preferred_element_type=jnp.float32).astype(
        jnp.bfloat16
    )
    split = vocab_count == 4
    if split:
        halves = half(partial_value)
        kept, sent = ordered(core == 1, halves[0], halves[1])
        pair = jnp.concatenate(ordered(core == 1, kept, across(sent, 1)), axis=1)
        parts = pair.reshape(2, span // 2, pair.shape[1])
        kept, sent = ordered(row == 1, parts[0], parts[1])
        mixed = jnp.concatenate(ordered(row == 1, kept, across(sent, 2)), axis=1)
    else:
        mixed = lax.all_gather(partial_value, "vocab", axis=1, tiled=True)
        mixed = half(mixed)
        mixed = jnp.where(core == 0, mixed[0], mixed[1])
    mtp_block = normalize(mixed, mtp_gain).astype(jnp.bfloat16)
    mtp_on = hops(mtp_block, onward, far - 1)
    mtp_back = hops(mtp_block, backward, far)

    place = jnp.int32(0)
    for i, s in enumerate(order):
        place = jnp.where(seq_index == s, i, place)
    sign = 1 - 2 * core

    def slot(distance):
        return (place - sign * distance) & (seq_count - 1)

    base_own = (seq_index * vocab_count + vocab_index) * block_cols
    base_peer = (seq_index * vocab_count + (vocab_index ^ 1)) * block_cols
    state = [
        jnp.zeros((3, 2 * seq_count, span), jnp.float32),
        jnp.zeros((2, 2 * seq_count, span), jnp.float32),
    ]

    def run(state, items):
        sources, blocks = [], []
        for head, _, parts in items:
            pieces = []
            for array, start, rows, where in parts:
                known = [i for i, s in enumerate(sources) if s is array]
                if not known:
                    sources.append(array)
                    known = [len(sources) - 1]
                pieces.append((known[0], start, rows, where))
            blocks.append((head, tuple(pieces)))
        scalars = jnp.stack([base_own, base_peer, row] + [slot(d) for _, d, _ in items])
        return head_stats(scalars, state, own, peer, block_cols, sources, tuple(blocks))

    def main_item(distance, block):
        return (0, distance, [(block, 0, span, 0)])

    def mtp_items(distances, blocks):
        if not split:
            return [(1, d, [(b, 0, span, 0)]) for d, b in zip(distances, blocks)]
        rows = span // 2
        other = across(jnp.concatenate(blocks) if len(blocks) > 1 else blocks[0], 2)
        return [
            (1, d, [(b, 0, rows, 1), (other, i * rows, rows, 2)])
            for i, (d, b) in enumerate(zip(distances, blocks))
        ]

    for k in range(1, far):
        state = run(state, [main_item(k, main_on[k - 1]), main_item(-k, main_back[k - 1])])
        if k == 1:
            state = run(state, [main_item(0, main_block)] + mtp_items([0], [mtp_block]))
        else:
            state = run(state, mtp_items([k - 1, 1 - k], [mtp_on[k - 2], mtp_back[k - 2]]))
    state = run(state, mtp_items([far - 1, 1 - far], [mtp_on[far - 2], mtp_back[far - 2]]))
    state = run(
        state, [main_item(far, main_on[far - 1])] + mtp_items([-far], [mtp_back[far - 1]])
    )
    stats, info = state

    bits = [("vocab", 2 << b) for b in range((vocab_count // 2).bit_length() - 1)]
    bits += [("seq", 1 << b) for b in range(seq_count.bit_length() - 1)]

    def swapped(value, chosen):
        masks = {"seq": 0, "vocab": 0}
        for axis, mask in chosen:
            masks[axis] ^= mask
        pairs = [
            (flat(s, v), flat(s ^ masks["seq"], v ^ masks["vocab"]))
            for s in range(seq_count)
            for v in range(vocab_count)
        ]
        return lax.ppermute(value, AXES, pairs)

    def is_set(bit):
        return (seq_index if bit[0] == "seq" else vocab_index) & bit[1] != 0

    for at in range(0, len(bits), 2):
        low, high = bits[at], bits[at + 1] if at + 1 < len(bits) else None
        near = swapped(stats, [low])
        if high is None:
            stats = join_stats(*ordered(is_set(low), stats, near))
        else:
            far_low, far_high = swapped(stats, [high]), swapped(stats, [low, high])
            here = ordered(is_set(low), stats, near)
            there = ordered(is_set(low), far_low, far_high)
            (a, c), (b, d) = (
                ordered(is_set(high), here[0], there[0]),
                ordered(is_set(high), here[1], there[1]),
            )
            stats = join_stats(join_stats(a, b), join_stats(c, d))

    losses = stats[0] + jnp.log(stats[1]) - stats[2]
    tokens = (info[1] * losses).reshape(2, seq_count, span)
    keeps = info[1].reshape(2, seq_count, span)
    at_own = jnp.arange(seq_count, dtype=jnp.int32)[:, None] == place
    shown = jnp.sum(jnp.where(at_own, tokens, 0.0), axis=1)
    packed = jnp.concatenate([shown, jnp.sum(tokens, axis=1), jnp.sum(keeps, axis=1)], axis=0)
    packed = jnp.stack(ordered(core == 1, packed, across(packed, 1)))
    main_tokens = packed[:, 0].reshape(batches, seq_len)
    mtp_tokens = packed[:, 1].reshape(batches, seq_len)
    sums = jnp.sum(packed[:, 2:], axis=(0, 2))
    total_loss = sums[0] / jnp.maximum(sums[2], 1.0) + MTP_WEIGHT * sums[1] / jnp.maximum(
        sums[3], 1.0
    )
    return (main_tokens, mtp_tokens, total_loss)


def solution(mesh):
    return jax.shard_map(
        functools.partial(shards, ring_order(mesh)),
        mesh=mesh,
        in_specs=(
            P(None, "seq", None),
            P(None, "seq", None),
            P(None, "seq"),
            P(None, "seq"),
            P(None, "seq"),
            P(),
            P(None, ("seq", "vocab")),
            P(None, "vocab"),
            P(),
            P(),
            P(),
            P(),
        ),
        out_specs=(P(None, "seq"), P(None, "seq"), P()),
        check_vma=False,
    )
```

time: 927 us -> 155 us (0.17)
  waiting for transfers between devices: 763 us -> 35 us
  Pallas kernels: 0 us -> 61.9 us
  matrix products: 51.1 us -> 1.24 us
  blocking collectives: 33.8 us -> 0 us
  other arithmetic: 40.7 us -> 10.1 us
  starting transfers between devices: 15.1 us -> 35.2 us
  between operations: 17.9 us -> 4.79 us
    all_gather x1 -> x0, waiting for transfers between devices: 574 us -> none  [shards(): mixed = lax.all_gather(partial_value, 'vocab', axis=1, tiled=True)]
    ppermute x8 -> x30, waiting for transfers between devices: 189 us -> 35 us  [the longest x14 21.6 us: hops(): block = lax.ppermute(block, AXES, pairs)]
    pallas_call x0 -> x8, Pallas kernels: none -> 61.9 us  [head_stats(): pl.pallas_call(functools.partial(head_kernel, blocks, valid, tile, len(so...]
    dot_general x1 -> x0, matrix products: 49.2 us -> none  [shards(): jnp.dot(jnp.concatenate([all_rows, partner], axis=0), held_cols, preferre...]
    psum x2 -> x0, blocking collectives: 28 us -> none  [the longest x1 22.3 us: shards(): summed = lax.psum((main_sum, mtp_sum), 'seq')]
    ppermute x8 -> x30, starting transfers between devices: 15 us -> 35.2 us  [the longest x14 14.4 us: hops(): block = lax.ppermute(block, AXES, pairs)]
    select_n x1 -> x7, other arithmetic: 15.6 us -> 0.17 us  [the longest x6 0.16 us: ordered(): return (jnp.where(swap, other, mine), jnp.where(swap, mine, other))]
    reduce_max x1 -> x0, other arithmetic: 9.4 us -> none  [column_stats(): highest = jnp.max(logits, axis=1)]
  transfers between devices with their start and end apart: 9 -> 30, of which waited for: 5 -> 11; matrix products, arithmetic and copies ran while one was open for 8% -> 7% of each run, Pallas kernels for 0% -> 35%
where the time goes in v1:
time: 155 us
  Pallas kernels  61.9 us (40%)
  starting transfers between devices  35.2 us (23%)
  waiting for transfers between devices  35 us (23%)
  other arithmetic  10.1 us (7%)
  local copies, waits for them, and re-layouts  6.59 us (4%)
  between operations  4.79 us (3%)
    pallas_call x8, Pallas kernels, head_stats(): pl.pallas_call(functools.partial(head_kernel, blocks, valid, tile, len(so...  61.9 us
    ppermute x14, waiting for transfers between devices, hops(): block = lax.ppermute(block, AXES, pairs)  21.6 us
    ppermute x14, starting transfers between devices, hops(): block = lax.ppermute(block, AXES, pairs)  14.4 us
    ppermute x6, starting transfers between devices, swapped(): return lax.ppermute(value, AXES, pairs)  8.01 us
    ppermute x9, starting transfers between devices, across(): return lax.ppermute(value, 'vocab', pairs)  7.98 us
    ppermute x9, waiting for transfers between devices, across(): return lax.ppermute(value, 'vocab', pairs)  7.04 us
    ppermute x6, waiting for transfers between devices, swapped(): return lax.ppermute(value, AXES, pairs)  6.37 us
    ppermute x1, starting transfers between devices, shards(): incoming = lax.ppermute(hidden[:, seq_len - 1:, :], 'seq', route)  4.87 us
  transfers between devices with their start and end apart: 30, of which 11 were waited for; matrix products, arithmetic and copies ran while one was open for 7% of the time, Pallas kernels for 35%

profile of v1, /device:TPU:0, one launch (start us, length us, event | category | flops | bytes accessed | tf_op | source)
XLA Modules:
  0.0 154.8 jit_solution(6872537919224944824)
XLA Ops:
  0.7 1.0 slice.143
  1.7 4.9 %collective-permute-start.3 = (bf16[2,1,2048]{2,1,0:T(2,128)(2,1)S(1)}, bf16[2,1,2048]{2,1,0:T(2,128)(2,1)S(1)}, u32[]{:S(2)}, u32[]{:S(2)}) collective-permute-start(bf16[2,1,2048]{2,1,0:T(2,128)(2,1)S(1)} %slice.143), channel_id=1, source_target_pairs={{0,4},{4,8},{8,12},{12,16},{16,20},{20,24},{24,28},{1,5},{5,9},{9,... | collective-permute-start | bytes 24584 | tf_op jit(solution)/shard_map/ppermute | solution.py:199
  6.6 1.5 fusion
  8.2 1.5 fusion.13
  9.7 1.0 fusion.15
  10.7 0.3 fusion.2
  11.2 0.4 multiply_reduce_fusion
  11.6 0.3 maximum_convert_fusion
  12.0 0.2 fusion.8
  12.2 1.6 %copy-done.11 = bf16[4096,512]{1,0:T(8,128)(2,1)S(1)} copy-done((bf16[4096,512]{1,0:T(8,128)(2,1)S(1)}, bf16[4096,512]{1,0:T(8,128)(2,1)}, u32[]{:S(2)}) %copy-start.11) | copy-done | bytes 4194328
  13.8 1.2 fusion.9
  15.1 0.6 collective-permute-start.4
  15.7 1.9 %collective-permute-done.4 = bf16[128,512]{1,0:T(8,128)(2,1)S(1)} collective-permute-done((bf16[128,512]{1,0:T(8,128)(2,1)S(1)}, bf16[128,512]{1,0:T(8,128)(2,1)S(1)}, u32[]{:S(2)}, u32[]{:S(2)}) %collective-permute-start.4) | collective-permute-done | bytes 131104 | tf_op jit(solution)/shard_map/ppermute | solution.py:190
  17.6 1.6 %collective-permute-start.5 = (bf16[64,1024]{1,0:T(8,128)(2,1)S(1)}, bf16[64,1024]{1,0:T(8,128)(2,1)S(1)}, u32[]{:S(2)}, u32[]{:S(2)}) collective-permute-start(bf16[64,1024]{1,0:T(8,128)(2,1)S(1)} %broadcast_select_fusion.7), channel_id=1, source_target_pairs={{0,2},{1,3},{2,0},{3,1},{4,6},{5,7},{6,4},{7,5},{8,10},{9,11},{10,... | collective-permute-start | bytes 393224 | tf_op jit(solution)/shard_map/ppermute | solution.py:190
  19.2 4.0 %collective-permute-done.5 = bf16[64,1024]{1,0:T(8,128)(2,1)S(1)} collective-permute-done((bf16[64,1024]{1,0:T(8,128)(2,1)S(1)}, bf16[64,1024]{1,0:T(8,128)(2,1)S(1)}, u32[]{:S(2)}, u32[]{:S(2)}) %collective-permute-start.5) | collective-permute-done | bytes 131104 | tf_op jit(solution)/shard_map/ppermute | solution.py:190
  23.3 0.2 fusion.17
  23.5 0.1 fusion.19.refs_6_
  23.6 1.6 %collective-permute-start.9 = (bf16[64,2048]{1,0:T(8,128)(2,1)S(1)}, bf16[64,2048]{1,0:T(8,128)(2,1)}, u32[]{:S(2)}, u32[]{:S(2)}) collective-permute-start(bf16[64,2048]{1,0:T(8,128)(2,1)S(1)} %fusion.19.refs_6_), channel_id=1, source_target_pairs={{0,4},{1,9},{2,6},{3,11},{4,12},{5,1},{6,14},{7,3},{8,0},{9,17},{1... | collective-permute-start | bytes 786440 | tf_op jit(solution)/shard_map/ppermute | solution.py:236
  25.2 0.5 collective-permute-start.10
  25.7 1.2 fusion.16.refs_5_
  26.9 1.6 %collective-permute-start.1 = (bf16[136,2048]{1,0:T(8,128)(2,1)S(1)}, bf16[136,2048]{1,0:T(8,128)(2,1)}, u32[]{:S(2)}, u32[]{:S(2)}) collective-permute-start(bf16[136,2048]{1,0:T(8,128)(2,1)S(1)} %fusion.16.refs_5_), channel_id=1, source_target_pairs={{0,4},{1,9},{2,6},{3,11},{4,12},{5,1},{6,14},{7,3},{8,0},{9,17},{1... | collective-permute-start | bytes 1671176 | tf_op jit(solution)/shard_map/ppermute | solution.py:236
  28.5 0.5 collective-permute-start.2
  29.0 3.9 %collective-permute-done.9.refs_5_ = bf16[64,2048]{1,0:T(8,128)(2,1)} collective-permute-done((bf16[64,2048]{1,0:T(8,128)(2,1)S(1)}, bf16[64,2048]{1,0:T(8,128)(2,1)}, u32[]{:S(2)}, u32[]{:S(2)}) %collective-permute-start.9) | collective-permute-done | bytes 262176 | tf_op jit(solution)/shard_map/ppermute | solution.py:236
  32.9 1.6 %collective-permute-start.14 = (bf16[64,2048]{1,0:T(8,128)(2,1)}, bf16[64,2048]{1,0:T(8,128)(2,1)S(1)}, u32[]{:S(2)}, u32[]{:S(2)}) collective-permute-start(bf16[64,2048]{1,0:T(8,128)(2,1)} %collective-permute-done.9.refs_5_), channel_id=1, source_target_pairs={{0,4},{1,9},{2,6},{3,11},{4,12},{5,1},{6,14},{7,3},{8,0},{9,17},{1... | collective-permute-start | bytes 786440 | tf_op jit(solution)/shard_map/ppermute | solution.py:236
  34.5 0.5 collective-permute-start.15
  35.4 14.6 %collective-permute-done.14.refs_5_ = bf16[64,2048]{1,0:T(8,128)(2,1)S(1)} collective-permute-done((bf16[64,2048]{1,0:T(8,128)(2,1)}, bf16[64,2048]{1,0:T(8,128)(2,1)S(1)}, u32[]{:S(2)}, u32[]{:S(2)}) %collective-permute-start.14) | collective-permute-done | bytes 262176 | tf_op jit(solution)/shard_map/ppermute | solution.py:236
  50.0 0.4 collective-permute-start.17
  50.5 1.6 %collective-permute-start.18 = (bf16[64,2048]{1,0:T(8,128)(2,1)}, bf16[64,2048]{1,0:T(8,128)(2,1)S(1)}, u32[]{:S(2)}, u32[]{:S(2)}) collective-permute-start(bf16[64,2048]{1,0:T(8,128)(2,1)} %collective-permute-done.15.refs_7_), channel_id=1, source_target_pairs={{4,0},{9,1},{6,2},{11,3},{12,4},{1,5},{14,6},{3,7},{0,8},{17,9},{2... | collective-permute-start | bytes 786440 | tf_op jit(solution)/shard_map/ppermute | solution.py:236
  52.0 1.1 pad_maximum_fusion
  53.1 0.5 collective-permute-start.7
  53.6 1.6 %collective-permute-start.8 = (bf16[136,2048]{1,0:T(8,128)(2,1)}, bf16[136,2048]{1,0:T(8,128)(2,1)S(1)}, u32[]{:S(2)}, u32[]{:S(2)}) collective-permute-start(bf16[136,2048]{1,0:T(8,128)(2,1)} %collective-permute-done.2.refs_6_), channel_id=1, source_target_pairs={{4,0},{9,1},{6,2},{11,3},{12,4},{1,5},{14,6},{3,7},{0,8},{17,9},{2... | collective-permute-start | bytes 1671176 | tf_op jit(solution)/shard_map/ppermute | solution.py:236
  55.2 1.0 pad_maximum_fusion.1
  56.2 3.0 %collective-permute-done.17.refs_5_ = bf16[64,2048]{1,0:T(8,128)(2,1)S(1)} collective-permute-done((bf16[64,2048]{1,0:T(8,128)(2,1)S(1)}, bf16[64,2048]{1,0:T(8,128)(2,1)S(1)}, u32[]{:S(2)}, u32[]{:S(2)}) %collective-permute-start.17) | collective-permute-done | bytes 262176 | tf_op jit(solution)/shard_map/ppermute | solution.py:236
  59.2 1.5 collective-permute-start.6
  60.7 0.7 collective-permute-start.11
  61.4 1.4 collective-permute-start.16
  62.9 2.9 %copy-done = bf16[2048,1600]{0,1:T(8,128)(2,1)S(1)} copy-done((bf16[2048,1600]{0,1:T(8,128)(2,1)S(1)}, bf16[2048,1600]{0,1:T(8,128)(2,1)}, u32[]{:S(2)}) %copy-start) | copy-done | bytes 6553624
  65.7 8.1 %head_256.8 = (f32[3,16,128]{2,1,0:T(8,128)S(1)}, f32[2,16,128]{2,1,0:T(8,128)S(1)}) custom-call(s32[5]{0:T(128)S(1)} %stack.132.refs_0_, f32[3,16,128]{2,1,0:T(8,128)S(1)} %broadcast_in_dim.13.refs_1_, f32[2,16,128]{2,1,0:T(8,128)S(1)} %broadcast_in_dim.14.refs_2_, bf16[1600,2048]{1,0:T(8,128)(2,1)S(1)} %bitcast.111, ...), custom_call_target="tpu_custom_call" | custom-call | flops 3355443200 | bytes 14155776 | tf_op jit(solution)/shard_map/head_256/pallas_call | solution.py:128
  73.8 1.6 %collective-permute-start.21 = (bf16[64,2048]{1,0:T(8,128)(2,1)S(1)}, bf16[64,2048]{1,0:T(8,128)(2,1)S(1)}, u32[]{:S(2)}, u32[]{:S(2)}) collective-permute-start(bf16[64,2048]{1,0:T(8,128)(2,1)S(1)} %collective-permute-done.18.refs_7_), channel_id=1, source_target_pairs={{4,0},{9,1},{6,2},{11,3},{12,4},{1,5},{14,6},{3,7},{0,8},{17,9},{2... | collective-permute-start | bytes 786440 | tf_op jit(solution)/shard_map/ppermute | solution.py:236
  75.4 0.5 collective-permute-start.12
  75.9 1.6 %collective-permute-start.13 = (bf16[136,2048]{1,0:T(8,128)(2,1)S(1)}, bf16[136,2048]{1,0:T(8,128)(2,1)S(1)}, u32[]{:S(2)}, u32[]{:S(2)}) collective-permute-start(bf16[136,2048]{1,0:T(8,128)(2,1)S(1)} %collective-permute-done.8.refs_6_), channel_id=1, source_target_pairs={{4,0},{9,1},{6,2},{11,3},{12,4},{1,5},{14,6},{3,7},{0,8},{17,9},{2... | collective-permute-start | bytes 1671176 | tf_op jit(solution)/shard_map/ppermute | solution.py:236
  77.5 7.7 %head_256.9 = (f32[3,16,128]{2,1,0:T(8,128)S(1)}, f32[2,16,128]{2,1,0:T(8,128)S(1)}) custom-call(s32[5]{0:T(128)S(1)} %stack.134.refs_0_, f32[3,16,128]{2,1,0:T(8,128)S(1)} %get-tuple-element.19.refs_1_, f32[2,16,128]{2,1,0:T(8,128)S(1)} %get-tuple-element.20.refs_2_, bf16[1600,2048]{1,0:T(8,128)(2,1)S(1)} %bitcast.114, ...), custom_call_target="tpu_custom_call" | custom-call | flops 3355443200 | bytes 14155776 | tf_op jit(solution)/shard_map/head_256/pallas_call | solution.py:128
  85.2 7.7 %head_256.10 = (f32[3,16,128]{2,1,0:T(8,128)S(1)}, f32[2,16,128]{2,1,0:T(8,128)S(1)}) custom-call(s32[5]{0:T(128)S(1)} %stack.129.refs_0_, f32[3,16,128]{2,1,0:T(8,128)S(1)} %get-tuple-element.21.refs_1_, f32[2,16,128]{2,1,0:T(8,128)S(1)} %get-tuple-element.22.refs_2_, bf16[1600,2048]{1,0:T(8,128)(2,1)S(1)} %bitcast.115, ...), custom_call_target="tpu_custom_call" | custom-call | flops 3355443200 | bytes 14155776 | tf_op jit(solution)/shard_map/head_256/pallas_call | solution.py:128
  92.9 0.7 collective-permute-start.19
  93.6 1.4 collective-permute-start.22
  95.0 0.4 collective-permute-start.20
  95.4 7.8 %head_256.11 = (f32[3,16,128]{2,1,0:T(8,128)S(1)}, f32[2,16,128]{2,1,0:T(8,128)S(1)}) custom-call(s32[5]{0:T(128)S(1)} %stack.132.refs_0_, f32[3,16,128]{2,1,0:T(8,128)S(1)} %get-tuple-element.23.refs_1_, f32[2,16,128]{2,1,0:T(8,128)S(1)} %get-tuple-element.24.refs_2_, bf16[1600,2048]{1,0:T(8,128)(2,1)S(1)} %bitcast.116, ...), custom_call_target="tpu_custom_call" | custom-call | flops 3355443200 | bytes 14155776 | tf_op jit(solution)/shard_map/head_256/pallas_call | solution.py:128
  103.2 7.7 %head_256.12 = (f32[3,16,128]{2,1,0:T(8,128)S(1)}, f32[2,16,128]{2,1,0:T(8,128)S(1)}) custom-call(s32[5]{0:T(128)S(1)} %stack.126.refs_0_, f32[3,16,128]{2,1,0:T(8,128)S(1)} %get-tuple-element.25.refs_1_, f32[2,16,128]{2,1,0:T(8,128)S(1)} %get-tuple-element.26.refs_2_, bf16[1600,2048]{1,0:T(8,128)(2,1)S(1)} %bitcast.117, ...), custom_call_target="tpu_custom_call" | custom-call | flops 3355443200 | bytes 14155776 | tf_op jit(solution)/shard_map/head_256/pallas_call | solution.py:128
  110.9 7.7 %head_256.13 = (f32[3,16,128]{2,1,0:T(8,128)S(1)}, f32[2,16,128]{2,1,0:T(8,128)S(1)}) custom-call(s32[5]{0:T(128)S(1)} %stack.129.refs_0_, f32[3,16,128]{2,1,0:T(8,128)S(1)} %get-tuple-element.27.refs_1_, f32[2,16,128]{2,1,0:T(8,128)S(1)} %get-tuple-element.28.refs_2_, bf16[1600,2048]{1,0:T(8,128)(2,1)S(1)} %bitcast.118, ...), custom_call_target="tpu_custom_call" | custom-call | flops 3355443200 | bytes 14155776 | tf_op jit(solution)/shard_map/head_256/pallas_call | solution.py:128
  118.6 7.7 %head_256.14 = (f32[3,16,128]{2,1,0:T(8,128)S(1)}, f32[2,16,128]{2,1,0:T(8,128)S(1)}) custom-call(s32[5]{0:T(128)S(1)} %stack.126.refs_0_, f32[3,16,128]{2,1,0:T(8,128)S(1)} %get-tuple-element.29.refs_1_, f32[2,16,128]{2,1,0:T(8,128)S(1)} %get-tuple-element.30.refs_2_, bf16[1600,2048]{1,0:T(8,128)(2,1)S(1)} %bitcast.119, ...), custom_call_target="tpu_custom_call" | custom-call | flops 3355443200 | bytes 14155776 | tf_op jit(solution)/shard_map/head_256/pallas_call | solution.py:128
  126.3 7.7 %head_256.15 = (f32[3,16,128]{2,1,0:T(8,128)S(1)}, f32[2,16,128]{2,1,0:T(8,128)S(1)}) custom-call(s32[5]{0:T(128)S(1)} %stack.123.refs_0_, f32[3,16,128]{2,1,0:T(8,128)S(1)} %get-tuple-element.31.refs_1_, f32[2,16,128]{2,1,0:T(8,128)S(1)} %get-tuple-element.32.refs_2_, bf16[1600,2048]{1,0:T(8,128)(2,1)S(1)} %bitcast.120, ...), custom_call_target="tpu_custom_call" | custom-call | flops 3355443200 | bytes 14155776 | tf_op jit(solution)/shard_map/head_256/pallas_call | solution.py:128
  134.0 1.7 %collective-permute-start.23 = (f32[3,16,128]{2,1,0:T(8,128)S(1)}, f32[3,16,128]{2,1,0:T(8,128)S(1)}, u32[]{:S(2)}, u32[]{:S(2)}) collective-permute-start(f32[3,16,128]{2,1,0:T(8,128)S(1)} %get-tuple-element.34), channel_id=1, source_target_pairs={{0,6},{1,7},{2,4},{3,5},{4,2},{5,3},{6,0},{7,1},{8,14},{9,15},{10,... | collective-permute-start | bytes 73736 | tf_op jit(solution)/shard_map/ppermute | solution.py:334
  135.7 0.5 collective-permute-start.24
  136.2 1.4 collective-permute-start.25
  137.5 1.2 collective-permute-done.23
  138.8 0.7 collective-permute-done.24
  139.5 0.5 collective-permute-done.25
  140.1 3.6 %collective-permute-start.26 = (f32[3,16,128]{2,1,0:T(8,128)S(1)}, f32[3,16,128]{2,1,0:T(8,128)S(1)}, u32[]{:S(2)}, u32[]{:S(2)}) collective-permute-start(f32[3,16,128]{2,1,0:T(8,128)S(1)} %pad_maximum_fusion.5), channel_id=1, source_target_pairs={{0,24},{1,25},{2,26},{3,27},{4,28},{5,29},{6,30},{7,31},{8,16},{9,... | collective-permute-start | bytes 73736 | tf_op jit(solution)/shard_map/ppermute | solution.py:334
  143.7 0.8 collective-permute-start.28
  144.5 1.2 collective-permute-done.26
  145.7 2.7 %collective-permute-done.27 = f32[3,16,128]{2,1,0:T(8,128)S(1)} collective-permute-done((f32[3,16,128]{2,1,0:T(8,128)S(1)}, f32[3,16,128]{2,1,0:T(8,128)S(1)}, u32[]{:S(2)}, u32[]{:S(2)}) %collective-permute-start.27) | collective-permute-done | bytes 24608 | tf_op jit(solution)/shard_map/ppermute | solution.py:334
  148.6 1.2 collective-permute-done.29
  150.0 0.6 maximum_bitcast_fusion
  150.5 0.6 fusion.56
  (83 shorter events, 1.3 us)
Async XLA Ops:
  0.6 9.1 %copy-start.1 = (bf16[2,128,2048]{2,1,0:T(8,128)(2,1)S(1)}, bf16[2,128,2048]{2,1,0:T(8,128)(2,1)}, u32[]{:S(2)}) copy-start(bf16[2,128,2048]{2,1,0:T(8,128)(2,1)} %param.12) | copy-start | bytes 3145732
  0.6 10.1 %copy-start.2 = (bf16[2,128,2048]{2,1,0:T(8,128)(2,1)S(1)}, bf16[2,128,2048]{2,1,0:T(8,128)(2,1)}, u32[]{:S(2)}) copy-start(bf16[2,128,2048]{2,1,0:T(8,128)(2,1)} %param.13) | copy-start | bytes 3145732
  0.7 9.1 %copy-start.3 = (f32[2048]{0:T(1024)S(1)}, f32[2048]{0:T(1024)}, u32[]{:S(2)}) copy-start(f32[2048]{0:T(1024)} %param.20) | copy-start | bytes 24580
  0.7 10.1 %copy-start.4 = (f32[2048]{0:T(1024)S(1)}, f32[2048]{0:T(1024)}, u32[]{:S(2)}) copy-start(f32[2048]{0:T(1024)} %param.22) | copy-start | bytes 24580
  1.7 9.5 %collective-permute-start.3 = (bf16[2,1,2048]{2,1,0:T(2,128)(2,1)S(1)}, bf16[2,1,2048]{2,1,0:T(2,128)(2,1)S(1)}, u32[]{:S(2)}, u32[]{:S(2)}) collective-permute-start(bf16[2,1,2048]{2,1,0:T(2,128)(2,1)S(1)} %slice.143), channel_id=1, source_target_pairs={{0,4},{4,8},{8,12},{12,16},{16,20},{20,24},{24,28},{1,5},{5,9},{9,... | collective-permute-start | bytes 24584 | tf_op jit(solution)/shard_map/ppermute | solution.py:199
  6.6 54.9 %collective-permute-start = (bf16[1600,2048]{1,0:T(8,128)(2,1)}, bf16[1600,2048]{1,0:T(8,128)(2,1)}, u32[]{:S(2)}, u32[]{:S(2)}) collective-permute-start(bf16[1600,2048]{1,0:T(8,128)(2,1)} %bitcast.110), channel_id=1, source_target_pairs={{0,1},{1,0},{2,3},{3,2},{4,5},{5,4},{6,7},{7,6},{8,9},{9,8},{10,11... | collective-permute-start | bytes 19660808 | tf_op jit(solution)/shard_map/ppermute | solution.py:190
  9.6 1.4 copy-start.8
  9.6 1.4 copy-start.9
  9.7 1.4 copy-start.10
  11.2 0.8 copy-start.5
  11.6 2.2 %copy-start.11 = (bf16[4096,512]{1,0:T(8,128)(2,1)S(1)}, bf16[4096,512]{1,0:T(8,128)(2,1)}, u32[]{:S(2)}) copy-start(bf16[4096,512]{1,0:T(8,128)(2,1)} %param.19) | copy-start | bytes 12582916
  13.8 1.8 %copy-start.7 = (s32[2,128]{1,0:T(2,128)S(1)}, s32[2,128]{1,0:T(2,128)}, u32[]{:S(2)}) copy-start(s32[2,128]{1,0:T(2,128)} %param.14) | copy-start | bytes 3076
  15.1 8.4 %copy-start.6 = (f32[2048]{0:T(1024)S(1)}, f32[2048]{0:T(1024)}, u32[]{:S(2)}) copy-start(f32[2048]{0:T(1024)} %param.23) | copy-start | bytes 24580
  15.1 2.5 %collective-permute-start.4 = (bf16[128,512]{1,0:T(8,128)(2,1)S(1)}, bf16[128,512]{1,0:T(8,128)(2,1)S(1)}, u32[]{:S(2)}, u32[]{:S(2)}) collective-permute-start(bf16[128,512]{1,0:T(8,128)(2,1)S(1)} %broadcast_select_fusion.3), channel_id=1, source_target_pairs={{0,1},{1,0},{2,3},{3,2},{4,5},{5,4},{6,7},{7,6},{8,9},{9,8},{10,11... | collective-permute-start | bytes 393224 | tf_op jit(solution)/shard_map/ppermute | solution.py:190
  17.6 5.6 %collective-permute-start.5 = (bf16[64,1024]{1,0:T(8,128)(2,1)S(1)}, bf16[64,1024]{1,0:T(8,128)(2,1)S(1)}, u32[]{:S(2)}, u32[]{:S(2)}) collective-permute-start(bf16[64,1024]{1,0:T(8,128)(2,1)S(1)} %broadcast_select_fusion.7), channel_id=1, source_target_pairs={{0,2},{1,3},{2,0},{3,1},{4,6},{5,7},{6,4},{7,5},{8,10},{9,11},{10,... | collective-permute-start | bytes 393224 | tf_op jit(solution)/shard_map/ppermute | solution.py:190
  23.6 9.3 %collective-permute-start.9 = (bf16[64,2048]{1,0:T(8,128)(2,1)S(1)}, bf16[64,2048]{1,0:T(8,128)(2,1)}, u32[]{:S(2)}, u32[]{:S(2)}) collective-permute-start(bf16[64,2048]{1,0:T(8,128)(2,1)S(1)} %fusion.19.refs_6_), channel_id=1, source_target_pairs={{0,4},{1,9},{2,6},{3,11},{4,12},{5,1},{6,14},{7,3},{8,0},{9,17},{1... | collective-permute-start | bytes 786440 | tf_op jit(solution)/shard_map/ppermute | solution.py:236
  25.2 9.3 %collective-permute-start.10 = (bf16[64,2048]{1,0:T(8,128)(2,1)S(1)}, bf16[64,2048]{1,0:T(8,128)(2,1)}, u32[]{:S(2)}, u32[]{:S(2)}) collective-permute-start(bf16[64,2048]{1,0:T(8,128)(2,1)S(1)} %fusion.19.refs_6_), channel_id=1, source_target_pairs={{4,0},{9,1},{6,2},{11,3},{12,4},{1,5},{14,6},{3,7},{0,8},{17,9},{2... | collective-permute-start | bytes 786440 | tf_op jit(solution)/shard_map/ppermute | solution.py:236
  25.7 51.8 %slice-start = ((s8[6553600]{0:T(1024)(128)(4,1)}), s8[2359296]{0:T(1024)(128)(4,1)S(1)}, s32[]{:S(2)}) async-start(s8[6553600]{0:T(1024)(128)(4,1)} %bitcast.112), calls=%async_computation | async-start | bytes 4718592
  26.9 26.2 %collective-permute-start.1 = (bf16[136,2048]{1,0:T(8,128)(2,1)S(1)}, bf16[136,2048]{1,0:T(8,128)(2,1)}, u32[]{:S(2)}, u32[]{:S(2)}) collective-permute-start(bf16[136,2048]{1,0:T(8,128)(2,1)S(1)} %fusion.16.refs_5_), channel_id=1, source_target_pairs={{0,4},{1,9},{2,6},{3,11},{4,12},{5,1},{6,14},{7,3},{8,0},{9,17},{1... | collective-permute-start | bytes 1671176 | tf_op jit(solution)/shard_map/ppermute | solution.py:236
  28.5 25.1 %collective-permute-start.2 = (bf16[136,2048]{1,0:T(8,128)(2,1)S(1)}, bf16[136,2048]{1,0:T(8,128)(2,1)}, u32[]{:S(2)}, u32[]{:S(2)}) collective-permute-start(bf16[136,2048]{1,0:T(8,128)(2,1)S(1)} %fusion.16.refs_5_), channel_id=1, source_target_pairs={{4,0},{9,1},{6,2},{11,3},{12,4},{1,5},{14,6},{3,7},{0,8},{17,9},{2... | collective-permute-start | bytes 1671176 | tf_op jit(solution)/shard_map/ppermute | solution.py:236
  32.9 17.1 %collective-permute-start.14 = (bf16[64,2048]{1,0:T(8,128)(2,1)}, bf16[64,2048]{1,0:T(8,128)(2,1)S(1)}, u32[]{:S(2)}, u32[]{:S(2)}) collective-permute-start(bf16[64,2048]{1,0:T(8,128)(2,1)} %collective-permute-done.9.refs_5_), channel_id=1, source_target_pairs={{0,4},{1,9},{2,6},{3,11},{4,12},{5,1},{6,14},{7,3},{8,0},{9,17},{1... | collective-permute-start | bytes 786440 | tf_op jit(solution)/shard_map/ppermute | solution.py:236
  34.5 16.0 %collective-permute-start.15 = (bf16[64,2048]{1,0:T(8,128)(2,1)}, bf16[64,2048]{1,0:T(8,128)(2,1)}, u32[]{:S(2)}, u32[]{:S(2)}) collective-permute-start(bf16[64,2048]{1,0:T(8,128)(2,1)} %collective-permute-done.10.refs_7_), channel_id=1, source_target_pairs={{4,0},{9,1},{6,2},{11,3},{12,4},{1,5},{14,6},{3,7},{0,8},{17,9},{2... | collective-permute-start | bytes 786440 | tf_op jit(solution)/shard_map/ppermute | solution.py:236
  50.0 9.2 %collective-permute-start.17 = (bf16[64,2048]{1,0:T(8,128)(2,1)S(1)}, bf16[64,2048]{1,0:T(8,128)(2,1)S(1)}, u32[]{:S(2)}, u32[]{:S(2)}) collective-permute-start(bf16[64,2048]{1,0:T(8,128)(2,1)S(1)} %collective-permute-done.14.refs_5_), channel_id=1, source_target_pairs={{0,4},{1,9},{2,6},{3,11},{4,12},{5,1},{6,14},{7,3},{8,0},{9,17},{1... | collective-permute-start | bytes 786440 | tf_op jit(solution)/shard_map/ppermute | solution.py:236
  50.5 10.3 %collective-permute-start.18 = (bf16[64,2048]{1,0:T(8,128)(2,1)}, bf16[64,2048]{1,0:T(8,128)(2,1)S(1)}, u32[]{:S(2)}, u32[]{:S(2)}) collective-permute-start(bf16[64,2048]{1,0:T(8,128)(2,1)} %collective-permute-done.15.refs_7_), channel_id=1, source_target_pairs={{4,0},{9,1},{6,2},{11,3},{12,4},{1,5},{14,6},{3,7},{0,8},{17,9},{2... | collective-permute-start | bytes 786440 | tf_op jit(solution)/shard_map/ppermute | solution.py:236
  53.1 22.3 %collective-permute-start.7 = (bf16[136,2048]{1,0:T(8,128)(2,1)}, bf16[136,2048]{1,0:T(8,128)(2,1)S(1)}, u32[]{:S(2)}, u32[]{:S(2)}) collective-permute-start(bf16[136,2048]{1,0:T(8,128)(2,1)} %collective-permute-done.1.refs_5_), channel_id=1, source_target_pairs={{0,4},{1,9},{2,6},{3,11},{4,12},{5,1},{6,14},{7,3},{8,0},{9,17},{1... | collective-permute-start | bytes 1671176 | tf_op jit(solution)/shard_map/ppermute | solution.py:236
  53.6 22.3 %collective-permute-start.8 = (bf16[136,2048]{1,0:T(8,128)(2,1)}, bf16[136,2048]{1,0:T(8,128)(2,1)S(1)}, u32[]{:S(2)}, u32[]{:S(2)}) collective-permute-start(bf16[136,2048]{1,0:T(8,128)(2,1)} %collective-permute-done.2.refs_6_), channel_id=1, source_target_pairs={{4,0},{9,1},{6,2},{11,3},{12,4},{1,5},{14,6},{3,7},{0,8},{17,9},{2... | collective-permute-start | bytes 1671176 | tf_op jit(solution)/shard_map/ppermute | solution.py:236
  59.2 14.6 %collective-permute-start.6 = (bf16[64,2048]{1,0:T(8,128)(2,1)S(1)}, bf16[64,2048]{1,0:T(8,128)(2,1)S(1)}, u32[]{:S(2)}, u32[]{:S(2)}) collective-permute-start(bf16[64,2048]{1,0:T(8,128)(2,1)S(1)} %fusion.19.refs_6_), channel_id=1, source_target_pairs={{0,2},{1,3},{2,0},{3,1},{4,6},{5,7},{6,4},{7,5},{8,10},{9,11},{10,... | collective-permute-start | bytes 786440 | tf_op jit(solution)/shard_map/ppermute | solution.py:190
  60.7 32.2 %collective-permute-start.11 = (bf16[128,2048]{1,0:T(8,128)(2,1)S(1)}, bf16[128,2048]{1,0:T(8,128)(2,1)S(1)}, u32[]{:S(2)}, u32[]{:S(2)}) collective-permute-start(bf16[128,2048]{1,0:T(8,128)(2,1)S(1)} %pad_maximum_fusion), channel_id=1, source_target_pairs={{0,2},{1,3},{2,0},{3,1},{4,6},{5,7},{6,4},{7,5},{8,10},{9,11},{10,... | collective-permute-start | bytes 1572872 | tf_op jit(solution)/shard_map/ppermute | solution.py:190
  61.4 49.5 %collective-permute-start.16 = (bf16[128,2048]{1,0:T(8,128)(2,1)S(1)}, bf16[128,2048]{1,0:T(8,128)(2,1)S(1)}, u32[]{:S(2)}, u32[]{:S(2)}) collective-permute-start(bf16[128,2048]{1,0:T(8,128)(2,1)S(1)} %pad_maximum_fusion.1), channel_id=1, source_target_pairs={{0,2},{1,3},{2,0},{3,1},{4,6},{5,7},{6,4},{7,5},{8,10},{9,11},{10,... | collective-permute-start | bytes 1572872 | tf_op jit(solution)/shard_map/ppermute | solution.py:190
  62.9 2.9 %copy-start = (bf16[2048,1600]{0,1:T(8,128)(2,1)S(1)}, bf16[2048,1600]{0,1:T(8,128)(2,1)}, u32[]{:S(2)}) copy-start(bf16[2048,1600]{0,1:T(8,128)(2,1)} %param.18) | copy-start | bytes 19660804
  65.7 11.7 %slice-start.1 = ((s8[6553600]{0:T(1024)(128)(4,1)}), s8[4194304]{0:T(1024)(128)(4,1)S(1)}, s32[]{:S(2)}) async-start(s8[6553600]{0:T(1024)(128)(4,1)} %bitcast.112), calls=%async_computation.1 | async-start | bytes 8388608
  73.8 19.8 %collective-permute-start.21 = (bf16[64,2048]{1,0:T(8,128)(2,1)S(1)}, bf16[64,2048]{1,0:T(8,128)(2,1)S(1)}, u32[]{:S(2)}, u32[]{:S(2)}) collective-permute-start(bf16[64,2048]{1,0:T(8,128)(2,1)S(1)} %collective-permute-done.18.refs_7_), channel_id=1, source_target_pairs={{4,0},{9,1},{6,2},{11,3},{12,4},{1,5},{14,6},{3,7},{0,8},{17,9},{2... | collective-permute-start | bytes 786440 | tf_op jit(solution)/shard_map/ppermute | solution.py:236
  75.4 19.5 %collective-permute-start.12 = (bf16[136,2048]{1,0:T(8,128)(2,1)S(1)}, bf16[136,2048]{1,0:T(8,128)(2,1)S(1)}, u32[]{:S(2)}, u32[]{:S(2)}) collective-permute-start(bf16[136,2048]{1,0:T(8,128)(2,1)S(1)} %collective-permute-done.7.refs_5_), channel_id=1, source_target_pairs={{0,4},{1,9},{2,6},{3,11},{4,12},{5,1},{6,14},{7,3},{8,0},{9,17},{1... | collective-permute-start | bytes 1671176 | tf_op jit(solution)/shard_map/ppermute | solution.py:236
  75.9 27.3 %collective-permute-start.13 = (bf16[136,2048]{1,0:T(8,128)(2,1)S(1)}, bf16[136,2048]{1,0:T(8,128)(2,1)S(1)}, u32[]{:S(2)}, u32[]{:S(2)}) collective-permute-start(bf16[136,2048]{1,0:T(8,128)(2,1)S(1)} %collective-permute-done.8.refs_6_), channel_id=1, source_target_pairs={{4,0},{9,1},{6,2},{11,3},{12,4},{1,5},{14,6},{3,7},{0,8},{17,9},{2... | collective-permute-start | bytes 1671176 | tf_op jit(solution)/shard_map/ppermute | solution.py:236
  92.9 25.7 %collective-permute-start.19 = (bf16[128,2048]{1,0:T(8,128)(2,1)S(1)}, bf16[128,2048]{1,0:T(8,128)(2,1)S(1)}, u32[]{:S(2)}, u32[]{:S(2)}) collective-permute-start(bf16[128,2048]{1,0:T(8,128)(2,1)S(1)} %pad_maximum_fusion.2), channel_id=1, source_target_pairs={{0,2},{1,3},{2,0},{3,1},{4,6},{5,7},{6,4},{7,5},{8,10},{9,11},{10,... | collective-permute-start | bytes 1572872 | tf_op jit(solution)/shard_map/ppermute | solution.py:190
  93.6 32.7 %collective-permute-start.22 = (bf16[64,2048]{1,0:T(8,128)(2,1)S(1)}, bf16[64,2048]{1,0:T(8,128)(2,1)S(1)}, u32[]{:S(2)}, u32[]{:S(2)}) collective-permute-start(bf16[64,2048]{1,0:T(8,128)(2,1)S(1)} %collective-permute-done.21.refs_6_), channel_id=1, source_target_pairs={{0,2},{1,3},{2,0},{3,1},{4,6},{5,7},{6,4},{7,5},{8,10},{9,11},{10,... | collective-permute-start | bytes 786440 | tf_op jit(solution)/shard_map/ppermute | solution.py:190
  95.0 31.3 %collective-permute-start.20 = (bf16[136,2048]{1,0:T(8,128)(2,1)S(1)}, bf16[136,2048]{1,0:T(8,128)(2,1)S(1)}, u32[]{:S(2)}, u32[]{:S(2)}) collective-permute-start(bf16[136,2048]{1,0:T(8,128)(2,1)S(1)} %collective-permute-done.12.refs_5_), channel_id=1, source_target_pairs={{0,4},{1,9},{2,6},{3,11},{4,12},{5,1},{6,14},{7,3},{8,0},{9,17},{1... | collective-permute-start | bytes 1671176 | tf_op jit(solution)/shard_map/ppermute | solution.py:236
  134.0 4.8 %collective-permute-start.23 = (f32[3,16,128]{2,1,0:T(8,128)S(1)}, f32[3,16,128]{2,1,0:T(8,128)S(1)}, u32[]{:S(2)}, u32[]{:S(2)}) collective-permute-start(f32[3,16,128]{2,1,0:T(8,128)S(1)} %get-tuple-element.34), channel_id=1, source_target_pairs={{0,6},{1,7},{2,4},{3,5},{4,2},{5,3},{6,0},{7,1},{8,14},{9,15},{10,... | collective-permute-start | bytes 73736 | tf_op jit(solution)/shard_map/ppermute | solution.py:334
  135.7 3.8 %collective-permute-start.24 = (f32[3,16,128]{2,1,0:T(8,128)S(1)}, f32[3,16,128]{2,1,0:T(8,128)S(1)}, u32[]{:S(2)}, u32[]{:S(2)}) collective-permute-start(f32[3,16,128]{2,1,0:T(8,128)S(1)} %get-tuple-element.34), channel_id=1, source_target_pairs={{0,4},{1,5},{2,6},{3,7},{4,0},{5,1},{6,2},{7,3},{8,12},{9,13},{10,... | collective-permute-start | bytes 73736 | tf_op jit(solution)/shard_map/ppermute | solution.py:334
  136.2 3.8 %collective-permute-start.25 = (f32[3,16,128]{2,1,0:T(8,128)S(1)}, f32[3,16,128]{2,1,0:T(8,128)S(1)}, u32[]{:S(2)}, u32[]{:S(2)}) collective-permute-start(f32[3,16,128]{2,1,0:T(8,128)S(1)} %get-tuple-element.34), channel_id=1, source_target_pairs={{0,2},{1,3},{2,0},{3,1},{4,6},{5,7},{6,4},{7,5},{8,10},{9,11},{10,... | collective-permute-start | bytes 73736 | tf_op jit(solution)/shard_map/ppermute | solution.py:334
  140.1 5.7 %collective-permute-start.26 = (f32[3,16,128]{2,1,0:T(8,128)S(1)}, f32[3,16,128]{2,1,0:T(8,128)S(1)}, u32[]{:S(2)}, u32[]{:S(2)}) collective-permute-start(f32[3,16,128]{2,1,0:T(8,128)S(1)} %pad_maximum_fusion.5), channel_id=1, source_target_pairs={{0,24},{1,25},{2,26},{3,27},{4,28},{5,29},{6,30},{7,31},{8,16},{9,... | collective-permute-start | bytes 73736 | tf_op jit(solution)/shard_map/ppermute | solution.py:334
  143.7 4.7 %collective-permute-start.27 = (f32[3,16,128]{2,1,0:T(8,128)S(1)}, f32[3,16,128]{2,1,0:T(8,128)S(1)}, u32[]{:S(2)}, u32[]{:S(2)}) collective-permute-start(f32[3,16,128]{2,1,0:T(8,128)S(1)} %pad_maximum_fusion.5), channel_id=1, source_target_pairs={{0,16},{1,17},{2,18},{3,19},{4,20},{5,21},{6,22},{7,23},{8,24},{9,... | collective-permute-start | bytes 73736 | tf_op jit(solution)/shard_map/ppermute | solution.py:334
  143.7 4.7 %collective-permute-start.28 = (f32[3,16,128]{2,1,0:T(8,128)S(1)}, f32[3,16,128]{2,1,0:T(8,128)S(1)}, u32[]{:S(2)}, u32[]{:S(2)}) collective-permute-start(f32[3,16,128]{2,1,0:T(8,128)S(1)} %pad_maximum_fusion.5), channel_id=1, source_target_pairs={{0,8},{1,9},{2,10},{3,11},{4,12},{5,13},{6,14},{7,15},{8,0},{9,1},... | collective-permute-start | bytes 73736 | tf_op jit(solution)/shard_map/ppermute | solution.py:334
  148.6 1.2 collective-permute-start.29

commit v2 on v1

v2 whole, which is shorter than its diff:
```python
import functools

import jax
import jax.numpy as jnp
from jax import lax
from jax.experimental import pallas as pl
from jax.experimental.pallas import tpu as pltpu
from jax.sharding import PartitionSpec as P


EPSILON = 1e-06
MTP_WEIGHT = 0.3
LOWEST = -1e30
META_ROWS = 8
ROW_ALIGN = 16
TILE_MAX = 800
VMEM_LIMIT = 4 * 1024 * 1024
VMEM_MOST = 56 * 1024 * 1024
AXES = ("seq", "vocab")


def normalize(values, gain_vec):
    values = values.astype(jnp.float32)
    mean_square = jnp.mean(values * values, axis=-1, keepdims=True)
    return values * lax.rsqrt(mean_square + EPSILON) * gain_vec


def column_tiles(cols):
    tile = max(
        t for t in range(ROW_ALIGN, min(cols, TILE_MAX) + 1, ROW_ALIGN) if cols % t == 0
    )
    even = [(start, tile) for start in range(0, cols, tile)]
    half = tile // 2
    if half % ROW_ALIGN:
        return even, even
    return even, even[:-1] + [(cols - tile, half), (cols - half, half)]


def ring_order(mesh):
    count = mesh.shape["seq"]
    coords = [getattr(d, "coords", None) for d in mesh.devices[:, 0]]
    across = len({c[0] for c in coords}) if all(c is not None for c in coords) else 2
    if count % across or across < 2 or (count // across) % 2:
        return list(range(count))
    deep = count // across
    walk = [(0, x) for x in range(across)]
    for z in range(1, deep):
        line = list(range(1, across))
        walk += [(z, x) for x in (line[::-1] if z % 2 else line)]
    walk += [(z, 0) for z in range(deep - 1, 0, -1)]
    return [z * across + x for z, x in walk]


def head_kernel(segments, valid, count, fetch, *refs):
    scalars, state_in, ids_in, own, peer = refs[:5]
    sources = refs[5 : 5 + count]
    state, ids_out, *rest = refs[5 + count :]
    if fetch:
        held, x, wanted, top, total, picked, first, second, sem = rest
        arrival = pltpu.make_async_copy(peer, held, sem)
        arrival.start()
        peer = held
    else:
        x, wanted, top, total, picked, first, second = rest
    span = x.shape[0] // len(segments)
    cols = own.shape[0]
    state[...] = state_in[...]
    ids_out[...] = ids_in[...]
    half = state.shape[1] // 2
    y, core = scalars[2], scalars[6]

    def slot_of(head, distance, batch):
        block = (scalars[3] - scalars[4] * distance) & (half // 2 - 1)
        return head * half + 2 * block + (core if batch is None else batch)

    for at, (head, distance, batch, meta, parts) in enumerate(segments):
        for ref, start, rows, place in parts:
            shift = (0, y * rows, (1 - y) * rows, 0)[place]
            to = pl.multiple_of(at * span + shift, rows)
            if place == 3:
                start = pl.multiple_of(core * rows, rows)
            x[pl.ds(to, rows), :] = sources[ref][pl.ds(start, rows), :]
        slot = pl.ds(slot_of(head, distance, batch), 1)
        if meta:
            below = slot_of(1, distance, batch)
            ref, start = meta
            fields = sources[ref][start : start + META_ROWS, :span].astype(jnp.float32)
            low, high = fields[:4], fields[4:8]
            if batch is None:
                fields = jnp.where(core == 0, low, high)
            else:
                fields = high if batch else low
            ids = fields[0:1] * 256.0 + fields[1:2]
            ids_out[slot, :] = ids
            ids_out[pl.ds(below, 1), :] = ids
            state[3, slot, :] = fields[2:3]
            state[3, pl.ds(below, 1), :] = fields[3:4]
        ids = ids_out[slot, :].astype(jnp.int32)
        ids = jnp.broadcast_to(ids, (8, span)) - lax.broadcasted_iota(jnp.int32, (8, span), 0)
        wanted[:, at * span : (at + 1) * span] = ids
    top[...] = jnp.full(top.shape, LOWEST, jnp.float32)
    total[...] = jnp.zeros(total.shape, jnp.float32)
    picked[...] = jnp.zeros(picked.shape, jnp.float32)

    def fold(held, start, tile, base):
        logits = held[:tile, :].reshape(tile // 8, 8, x.shape[0])
        if valid < cols:
            place = lax.broadcasted_iota(jnp.int32, logits.shape, 0) * 8
            place += lax.broadcasted_iota(jnp.int32, logits.shape, 1)
            logits = jnp.where(place + start < valid, logits, LOWEST)
        old = top[...]
        new = jnp.maximum(old, jnp.max(logits, axis=0))
        top[...] = new
        offset = wanted[...] - (base + start)
        fresh = total[...] * jnp.exp(old - new)
        chosen = picked[...]
        for i in range(tile // 8):
            fresh += jnp.exp(logits[i] - new)
            reached = offset == 8 * i
            if valid < cols:
                reached &= logits[i] > LOWEST
            chosen = jnp.where(reached, logits[i], chosen)
        total[...] = fresh
        picked[...] = chosen

    waiting = None
    at = 0
    own_tiles, peer_tiles = column_tiles(cols)
    for weights, base, tiles in ((own, scalars[0], own_tiles), (peer, scalars[1], peer_tiles)):
        if fetch and weights is peer:
            arrival.wait()
        for start, tile in tiles:
            space = (first, second)[at % 2]
            space[:tile, :] = lax.dot_general(
                weights[start : start + tile, :],
                x[...],
                (((1,), (1,)), ((), ())),
                preferred_element_type=jnp.float32,
            )
            if waiting:
                fold(*waiting)
            waiting = (space, start, tile, base)
            at += 1
    fold(*waiting)
    highest = jnp.max(top[...], axis=0, keepdims=True)
    sums = jnp.sum(total[...] * jnp.exp(top[...] - highest), axis=0, keepdims=True)
    chosen = jnp.sum(picked[...], axis=0, keepdims=True)
    for at, (head, distance, batch, _, _) in enumerate(segments):
        lanes = slice(at * span, (at + 1) * span)
        slot = pl.ds(slot_of(head, distance, batch), 1)
        state[0, slot, :] = highest[:, lanes]
        state[1, slot, :] = sums[:, lanes]
        state[2, slot, :] = chosen[:, lanes]


def head_stats(scalars, state, own, peer, valid, sources, segments, fetch):
    cols, width = own.shape
    tile = column_tiles(cols)[0][0][1]
    span = state[0].shape[2]
    rows = len(segments) * span
    vmem = pl.BlockSpec(memory_space=pltpu.VMEM)
    wide = pltpu.VMEM((8, rows), jnp.float32)
    spaces = [
        pltpu.VMEM((rows, width), jnp.bfloat16),
        pltpu.VMEM((8, rows), jnp.int32),
        wide,
        wide,
        wide,
        pltpu.VMEM((tile, rows), jnp.float32),
        pltpu.VMEM((tile, rows), jnp.float32),
    ]
    peer_spec = pl.BlockSpec(memory_space=pltpu.HBM) if fetch else vmem
    kept = [*state, peer] if fetch else state
    return pl.pallas_call(
        functools.partial(head_kernel, segments, valid, len(sources), fetch),
        in_specs=[pl.BlockSpec(memory_space=pltpu.SMEM), vmem, vmem, vmem, peer_spec]
        + [vmem] * len(sources),
        out_specs=[vmem] * len(kept),
        out_shape=[jax.ShapeDtypeStruct(s.shape, s.dtype) for s in kept],
        scratch_shapes=spaces + [pltpu.SemaphoreType.DMA] * fetch,
        compiler_params=pltpu.CompilerParams(vmem_limit_bytes=VMEM_LIMIT),
        cost_estimate=pl.CostEstimate(
            flops=4 * rows * cols * width,
            bytes_accessed=4 * cols * width + 2 * rows * width,
            transcendentals=2 * rows * cols,
        ),
    )(scalars, *state, own, peer, *sources)


def normal_rows(values, gain):
    values = values.astype(jnp.float32)
    mean_square = jnp.mean(values * values, axis=-1, keepdims=True)
    return (values * lax.rsqrt(mean_square + EPSILON) * gain).astype(jnp.bfloat16)


def main_kernel(parts, scalars, lengths, hidden, gain, targets, main_mask, mtp_mask, *refs):
    block, rows, gains, ids, mains, mtps, sems = refs
    batches, share, width = rows.shape
    seq_len = share * parts
    y, first_position = scalars[2], scalars[5]
    start = pl.multiple_of(y * share, share) if parts > 1 else 0
    pairs = [(hidden.at[:, pl.ds(start, share)], rows), (gain, gains)]
    pairs += [(targets, ids), (main_mask, mains), (mtp_mask, mtps)]
    copies = [pltpu.make_async_copy(a, b, sems.at[i]) for i, (a, b) in enumerate(pairs)]
    for copy in copies:
        copy.start()
    for copy in copies:
        copy.wait()
    place = lax.broadcasted_iota(jnp.int32, (1, seq_len), 1) + first_position
    fields = []
    for batch in range(batches):
        block[batch * share : (batch + 1) * share, :] = normal_rows(rows[batch], gains[...])
        here = slice(batch, batch + 1)
        inside = place + 1 < lengths[batch]
        keep_main = (mains[here, :] == 1) & inside
        keep_mtp = (mtps[here, :] == 1) & inside & (place >= 1)
        digits = [ids[here, :] >> 8, ids[here, :] & 255]
        fields += [d.astype(jnp.float32) for d in digits]
        fields += [jnp.where(k, 1.0, 0.0) for k in (keep_main, keep_mtp)]
    below = slice(batches * share, batches * share + META_ROWS)
    block[below, :seq_len] = jnp.concatenate(fields, axis=0).astype(jnp.bfloat16)
    block[below, seq_len:] = jnp.zeros((META_ROWS, width - seq_len), jnp.bfloat16)


def main_rows_below(parts, scalars, lengths, hidden, gain, targets, main_mask, mtp_mask):
    batches, seq_len, width = hidden.shape
    smem = pl.BlockSpec(memory_space=pltpu.SMEM)
    far = pl.BlockSpec(memory_space=pltpu.HBM)
    whole = pltpu.VMEM((batches, seq_len), jnp.int32)
    shape = (batches * seq_len // parts + META_ROWS, width)
    return pl.pallas_call(
        functools.partial(main_kernel, parts),
        in_specs=[smem, smem] + [far] * 5,
        out_specs=pl.BlockSpec(memory_space=pltpu.VMEM),
        out_shape=jax.ShapeDtypeStruct(shape, jnp.bfloat16),
        scratch_shapes=[
            pltpu.VMEM((batches, seq_len // parts, width), jnp.bfloat16),
            pltpu.VMEM(gain.shape, jnp.float32),
            whole,
            whole,
            whole,
            pltpu.SemaphoreType.DMA((5,)),
        ],
        compiler_params=pltpu.CompilerParams(vmem_limit_bytes=VMEM_MOST),
        cost_estimate=pl.CostEstimate(
            flops=2 * batches * seq_len * width, bytes_accessed=hidden.size, transcendentals=0
        ),
        name="main_rows",
    )(scalars, lengths, hidden, gain, targets, main_mask, mtp_mask)


def mine_kernel(scalars, hidden, gain, mine):
    mine[...] = normal_rows(hidden[scalars[6]], gain[...])


def main_rows_mine(scalars, hidden, gain):
    vmem = pl.BlockSpec(memory_space=pltpu.VMEM)
    shape = hidden.shape[1:]
    return pl.pallas_call(
        mine_kernel,
        in_specs=[pl.BlockSpec(memory_space=pltpu.SMEM), vmem, vmem],
        out_specs=vmem,
        out_shape=jax.ShapeDtypeStruct(shape, jnp.bfloat16),
        compiler_params=pltpu.CompilerParams(vmem_limit_bytes=VMEM_LIMIT),
        cost_estimate=pl.CostEstimate(
            flops=2 * shape[0] * shape[1], bytes_accessed=hidden.size, transcendentals=0
        ),
        name="mine",
    )(scalars, hidden, gain)


def half_kernel(share, below, scalars, block, half):
    start = pl.multiple_of(scalars[6] * share, share)
    half[:share, :] = block[pl.ds(start, share), :]
    if below:
        half[share:, :] = block[2 * share :, :]


def half_of(scalars, block, share, below):
    vmem = pl.BlockSpec(memory_space=pltpu.VMEM)
    shape = (share + below, block.shape[1])
    return pl.pallas_call(
        functools.partial(half_kernel, share, below),
        in_specs=[pl.BlockSpec(memory_space=pltpu.SMEM), vmem],
        out_specs=vmem,
        out_shape=jax.ShapeDtypeStruct(shape, block.dtype),
        compiler_params=pltpu.CompilerParams(vmem_limit_bytes=VMEM_LIMIT),
        cost_estimate=pl.CostEstimate(
            flops=0, bytes_accessed=4 * shape[0] * shape[1], transcendentals=0
        ),
        name="half",
    )(scalars, block)


def mix_kernel(hidden, incoming, first_gain, embedded, second_gain, projection, out, *held):
    earlier, before, first_scale, tokens, second_scale, weights, joined, sems = held
    batches, seq_len, width = earlier.shape
    pairs = [(hidden, earlier), (incoming, before), (first_gain, first_scale)]
    pairs += [(embedded, tokens), (second_gain, second_scale), (projection, weights)]
    copies = [pltpu.make_async_copy(a, b, sems.at[i]) for i, (a, b) in enumerate(pairs)]
    for copy in copies:
        copy.start()

    def normal(values, gain):
        values = values.astype(jnp.float32)
        mean_square = jnp.mean(values * values, axis=-1, keepdims=True)
        return values * lax.rsqrt(mean_square + EPSILON) * gain

    for copy in copies[:3]:
        copy.wait()
    top = lax.broadcasted_iota(jnp.int32, (seq_len, width), 0) == 0
    for batch in range(batches):
        rows = slice(batch * seq_len, (batch + 1) * seq_len)
        shifted = pltpu.roll(normal(earlier[batch], first_scale[...]), 1, 0)
        shifted = jnp.where(top, normal(before[batch], first_scale[...]), shifted)
        joined[rows, :width] = shifted.astype(jnp.bfloat16)
    copies[3].wait()
    copies[4].wait()
    for batch in range(batches):
        rows = slice(batch * seq_len, (batch + 1) * seq_len)
        joined[rows, width:] = normal(tokens[batch], second_scale[...]).astype(jnp.bfloat16)
    copies[5].wait()
    out[...] = jnp.dot(
        joined[...], weights[...], preferred_element_type=jnp.float32
    ).astype(jnp.bfloat16)


def projected(*operands):
    hidden, projection = operands[0], operands[-1]
    batches, seq_len, width = hidden.shape
    rows, cols = batches * seq_len, projection.shape[1]
    far = pl.BlockSpec(memory_space=pltpu.HBM)
    return pl.pallas_call(
        mix_kernel,
        in_specs=[far] * len(operands),
        out_specs=pl.BlockSpec(memory_space=pltpu.VMEM),
        out_shape=jax.ShapeDtypeStruct((rows, cols), jnp.bfloat16),
        scratch_shapes=[pltpu.VMEM(a.shape, a.dtype) for a in operands]
        + [pltpu.VMEM((rows, 2 * width), jnp.bfloat16), pltpu.SemaphoreType.DMA((6,))],
        compiler_params=pltpu.CompilerParams(vmem_limit_bytes=VMEM_MOST),
        cost_estimate=pl.CostEstimate(
            flops=4 * rows * width * cols, bytes_accessed=2 * projection.size, transcendentals=0
        ),
        name="mix",
    )(*operands)


def arrange_kernel(scalars, mine, beside, above, across, gain, out):
    width = out.shape[1]
    part = width // 4
    y, core = scalars[2], scalars[6]
    quarters = [(mine, y, core), (beside, y, 1 - core)]
    quarters += [(above, 1 - y, core), (across, 1 - y, 1 - core)]
    square = 0.0
    for quarter, _, _ in quarters:
        values = quarter[...].astype(jnp.float32)
        square += jnp.sum(values * values, axis=-1, keepdims=True)
    scale = lax.rsqrt(square / width + EPSILON)
    for quarter, at_y, at_core in quarters:
        lanes = pl.ds(pl.multiple_of((2 * at_y + at_core) * part, part), part)
        values = quarter[...].astype(jnp.float32) * scale * gain[:, lanes]
        out[:, lanes] = values.astype(jnp.bfloat16)


def arranged(scalars, quarters, gain):
    rows, width = quarters[0].shape[0], gain.shape[1]
    vmem = pl.BlockSpec(memory_space=pltpu.VMEM)
    return pl.pallas_call(
        arrange_kernel,
        in_specs=[pl.BlockSpec(memory_space=pltpu.SMEM)] + [vmem] * 5,
        out_specs=vmem,
        out_shape=jax.ShapeDtypeStruct((rows, width), jnp.bfloat16),
        compiler_params=pltpu.CompilerParams(vmem_limit_bytes=VMEM_LIMIT),
        cost_estimate=pl.CostEstimate(
            flops=4 * rows * width, bytes_accessed=4 * rows * width, transcendentals=rows
        ),
        name="arrange",
    )(scalars, *quarters, gain)


def join_stats(earlier, latter):
    highest = jnp.maximum(earlier[0], latter[0])
    exp_total = earlier[1] * jnp.exp(earlier[0] - highest)
    exp_total += latter[1] * jnp.exp(latter[0] - highest)
    return jnp.stack([highest, exp_total, earlier[2] + latter[2]])


def ordered(swap, mine, other):
    return jnp.where(swap, other, mine), jnp.where(swap, mine, other)


def shards(
    order,
    hidden,
    embedded,
    targets,
    main_mask,
    mtp_mask,
    lengths,
    head_weight,
    projection,
    main_gain,
    hidden_gain,
    embed_gain,
    mtp_gain,
):
    batches, seq_len, _ = hidden.shape
    seq_index = lax.axis_index("seq")
    vocab_index = lax.axis_index("vocab")
    seq_count = lax.axis_size("seq")
    vocab_count = lax.axis_size("vocab")
    core = vocab_index & 1
    row = vocab_index >> 1
    block_cols = head_weight.shape[1]
    parts = 2 if vocab_count == 4 else 1
    share = seq_len // parts
    far = seq_count // 2

    def across(value, mask):
        pairs = [(v, v ^ mask) for v in range(vocab_count)]
        return lax.ppermute(value, "vocab", pairs)

    own = head_weight.T
    padding = -block_cols % ROW_ALIGN
    if padding:
        own = jnp.pad(own, ((0, padding), (0, 0)))
    peer = across(own, 1)
    route = [(i - 1, i) for i in range(1, seq_count)]
    incoming = lax.ppermute(hidden[:, seq_len - 1 :, :], "seq", route)

    place = jnp.int32(0)
    for i, s in enumerate(order):
        place = jnp.where(seq_index == s, i, place)
    base_own = (seq_index * vocab_count + vocab_index) * block_cols
    base_peer = (seq_index * vocab_count + (vocab_index ^ 1)) * block_cols
    scalars = jnp.stack(
        [base_own, base_peer, row, place, 1 - 2 * core, seq_index * seq_len, core]
    )

    gain_row = main_gain.reshape(1, -1)
    main_block = main_rows_below(
        parts, scalars, lengths, hidden, gain_row, targets, main_mask, mtp_mask
    )
    main_mine = main_rows_mine(scalars, hidden, gain_row)

    def flat(s, v):
        return s * vocab_count + v

    following = {s: order[(i + 1) % seq_count] for i, s in enumerate(order)}
    leading = {b: a for a, b in following.items()}
    onward = [
        (flat(s, v), flat((leading if v & 1 else following)[s], v))
        for s in range(seq_count)
        for v in range(vocab_count)
    ]

    def hops(block, half):
        found = []
        for at in range(1, far + 1):
            if at == far:
                block = half(block)
            block = lax.ppermute(block, AXES, onward)
            found.append(block)
        return found

    def main_half(block):
        return half_of(scalars, block, share, META_ROWS)

    main_hops = hops(main_block, main_half)
    main_others = [across(block, 2) if parts > 1 else None for block in main_hops]

    partial_value = projected(
        hidden,
        incoming,
        hidden_gain.reshape(1, -1),
        embedded,
        embed_gain.reshape(1, -1),
        projection,
    )
    if parts > 1:
        beside = across(partial_value, 1)
        above = across(partial_value, 2)
        quarters = (partial_value, beside, above, across(above, 1))
        mtp_block = arranged(scalars, quarters, mtp_gain.reshape(1, -1))
    else:
        mixed = lax.all_gather(partial_value, "vocab", axis=1, tiled=True)
        mtp_block = normalize(mixed, mtp_gain).astype(jnp.bfloat16)

    def mtp_half(block):
        return half_of(scalars, block, seq_len, 0)

    mtp_hops = hops(mtp_block, mtp_half)

    slots = 4 * seq_count
    empty = [LOWEST, 0.0, 0.0, 0.0]
    state = [
        jnp.stack([jnp.full((slots, seq_len), e, jnp.float32) for e in empty]),
        jnp.zeros((slots, seq_len), jnp.float32),
    ]
    columns = [own, peer]

    def run(state, segments, fetch=False):
        sources = []

        def number(array):
            known = [i for i, s in enumerate(sources) if s is array]
            if not known:
                sources.append(array)
                known = [len(sources) - 1]
            return known[0]

        known = []
        for head, distance, batch, meta, pieces in segments:
            pieces = tuple((number(p[0]),) + p[1:] for p in pieces)
            meta = (number(meta[0]), meta[1]) if meta else None
            known.append((head, distance, batch, meta, pieces))
        out = head_stats(
            scalars, state, *columns, block_cols, sources, tuple(known), fetch
        )
        if fetch:
            columns[1] = out[2]
        return out[:2]

    def main_segment(at, batch):
        block, other = main_hops[at - 1], main_others[at - 1]
        start = 0 if at == far else batch * share
        pieces = [(block, start, share, 1 if parts > 1 else 0)]
        if parts > 1:
            pieces.append((other, start, share, 2))
        meta = (block, share if at == far else 2 * share)
        return (0, at, batch, meta, pieces)

    def main_pair(at):
        return [main_segment(at, batch) for batch in range(2)]

    def mtp_pair(at):
        meta = (main_hops[at - 1], 2 * share)
        return [
            (1, at, batch, meta, [(mtp_hops[at - 1], batch * seq_len, seq_len, 0)])
            for batch in range(2)
        ]

    own_rows = [
        (0, 0, None, (main_block, 2 * share), [(main_mine, 0, seq_len, 0)]),
        (1, 0, None, None, [(mtp_block, 0, seq_len, 3)]),
    ]
    state = run(state, own_rows, True)
    for at in range(1, far):
        state = run(state, mtp_pair(at))
        state = run(state, main_pair(at))
    last_rows = [
        main_segment(far, None),
        (1, far, None, None, [(mtp_hops[far - 1], 0, seq_len, 0)]),
    ]
    stats, _ = run(state, last_rows)

    bits = [("vocab", 2 << b) for b in range((vocab_count // 2).bit_length() - 1)]
    bits += [("seq", 1 << b) for b in range(seq_count.bit_length() - 1)]

    def swapped(value, chosen):
        masks = {"seq": 0, "vocab": 0}
        for axis, mask in chosen:
            masks[axis] ^= mask
        pairs = [
            (flat(s, v), flat(s ^ masks["seq"], v ^ masks["vocab"]))
            for s in range(seq_count)
            for v in range(vocab_count)
        ]
        return lax.ppermute(value, AXES, pairs)

    def is_set(bit):
        return (seq_index if bit[0] == "seq" else vocab_index) & bit[1] != 0

    stats, others = ordered(core == 1, stats, swapped(stats, [("vocab", 1)]))
    keeps = stats[3] + others[3]
    stats = join_stats(stats, others)
    for at in range(0, len(bits), 2):
        low, high = bits[at], bits[at + 1] if at + 1 < len(bits) else None
        near = swapped(stats, [low])
        if high is None:
            stats = join_stats(*ordered(is_set(low), stats, near))
        else:
            far_low, far_high = swapped(stats, [high]), swapped(stats, [low, high])
            here = ordered(is_set(low), stats, near)
            there = ordered(is_set(low), far_low, far_high)
            (a, c), (b, d) = (
                ordered(is_set(high), here[0], there[0]),
                ordered(is_set(high), here[1], there[1]),
            )
            stats = join_stats(join_stats(a, b), join_stats(c, d))

    losses = stats[0] + jnp.log(stats[1]) - stats[2]
    tokens = (keeps * losses).reshape(2, seq_count, batches, seq_len)
    keeps = keeps.reshape(2, seq_count, batches, seq_len)
    shown = lax.dynamic_index_in_dim(tokens, place, axis=1, keepdims=False)
    sums = jnp.sum(tokens, axis=(1, 2, 3))
    counts = jnp.maximum(jnp.sum(keeps, axis=(1, 2, 3)), 1.0)
    total_loss = sums[0] / counts[0] + MTP_WEIGHT * sums[1] / counts[1]
    return (shown[0], shown[1], total_loss)


def solution(mesh):
    return jax.shard_map(
        functools.partial(shards, ring_order(mesh)),
        mesh=mesh,
        in_specs=(
            P(None, "seq", None),
            P(None, "seq", None),
            P(None, "seq"),
            P(None, "seq"),
            P(None, "seq"),
            P(),
            P(None, ("seq", "vocab")),
            P(None, "vocab"),
            P(),
            P(),
            P(),
            P(),
        ),
        out_specs=(P(None, "seq"), P(None, "seq"), P()),
        check_vma=False,
    )
```

time: 155 us -> 170 us (1.097)
  waiting for transfers between devices: 35 us -> 72.3 us
  other arithmetic: 10.1 us -> 0.56 us
  Pallas kernels: 61.9 us -> 53.1 us
  starting transfers between devices: 35.2 us -> 29.5 us
  local copies, waits for them, and re-layouts: 6.59 us -> 9.07 us
    ppermute x14 -> x8, waiting for transfers between devices: 21.6 us -> 53.6 us  [hops(): block = lax.ppermute(block, AXES, onward)]
    pallas_call x8 -> x14, Pallas kernels: 61.9 us -> 53.1 us  [the longest x8 41.5 us: head_stats(): pl.pallas_call(functools.partial(head_kernel, segments, valid, len(source...]
    ppermute x14 -> x8, starting transfers between devices: 14.4 us -> 10.7 us  [hops(): block = lax.ppermute(block, AXES, onward)]
    reduce_sum x6 -> x3, other arithmetic: 3.77 us -> 0.37 us  [the longest x2 0.25 us: shards(): counts = jnp.maximum(jnp.sum(keeps, axis=(1, 2, 3)), 1.0)]
    concatenate x5 -> x0, other arithmetic: 3.34 us -> none  [the longest x3 2.1 us: mtp_items(): other = across(jnp.concatenate(blocks) if len(blocks) > 1 else blocks[0], 2)]
    ppermute x6 -> x7, waiting for transfers between devices: 6.37 us -> 8.88 us  [swapped(): return lax.ppermute(value, AXES, pairs)]
    unnamed x28 -> x30, local copies, waits for them, and re-layouts: 4.54 us -> 6.78 us
    ppermute x9 -> x8, starting transfers between devices: 7.98 us -> 6.27 us  [across(): return lax.ppermute(value, 'vocab', pairs)]
  transfers between devices with their start and end apart: 30 -> 24, of which waited for: 11 -> 14; matrix products, arithmetic and copies ran while one was open for 7% -> 1% of each run, Pallas kernels for 35% -> 28%
where the time goes in v2:
time: 170 us; the launch traced here: 169 us
  waiting for transfers between devices  72.3 us (43%)
  Pallas kernels  53.1 us (31%)
  starting transfers between devices  29.5 us (17%)
  local copies, waits for them, and re-layouts  9.07 us (5%)
  between operations  4.66 us (3%)
    ppermute x8, waiting for transfers between devices, hops(): block = lax.ppermute(block, AXES, onward)  53.6 us
    pallas_call x8, Pallas kernels, head_stats(): pl.pallas_call(functools.partial(head_kernel, segments, valid, len(source...  41.5 us
    ppermute x8, starting transfers between devices, hops(): block = lax.ppermute(block, AXES, onward)  10.7 us
    ppermute x7, waiting for transfers between devices, swapped(): return lax.ppermute(value, AXES, pairs)  8.88 us
    ppermute x8, waiting for transfers between devices, across(): return lax.ppermute(value, 'vocab', pairs)  8.37 us
    ppermute x7, starting transfers between devices, swapped(): return lax.ppermute(value, AXES, pairs)  8.01 us
    unnamed x30, local copies, waits for them, and re-layouts  6.78 us
    ppermute x8, starting transfers between devices, across(): return lax.ppermute(value, 'vocab', pairs)  6.27 us
  transfers between devices with their start and end apart: 24, of which 14 were waited for; matrix products, arithmetic and copies ran while one was open for 1% of the time, Pallas kernels for 28%

profile of v2, /device:TPU:0, one launch (start us, length us, event | category | flops | bytes accessed | tf_op | source)
XLA Modules:
  0.0 169.1 jit_solution(3719857752036785778)
XLA Ops:
  0.7 0.6 collective-permute-start
  1.2 0.9 slice.129
  2.1 4.5 %collective-permute-start.1 = (bf16[2,1,2048]{2,1,0:T(2,128)(2,1)S(1)}, bf16[2,1,2048]{2,1,0:T(2,128)(2,1)S(1)}, u32[]{:S(2)}, u32[]{:S(2)}) collective-permute-start(bf16[2,1,2048]{2,1,0:T(2,128)(2,1)S(1)} %slice.129), channel_id=1, source_target_pairs={{0,4},{4,8},{8,12},{12,16},{16,20},{20,24},{24,28},{1,5},{5,9},{9,... | collective-permute-start | bytes 24584 | tf_op jit(solution)/shard_map/ppermute | solution.py:429
  6.6 1.4 collective-permute-done.1.incoming
  8.0 0.6 copy-done.12
  8.6 5.0 %mix.1.mine = bf16[256,512]{1,0:T(8,128)(2,1)} custom-call(bf16[2,128,2048]{2,1,0:T(8,128)(2,1)} %hidden.5, bf16[2,1,2048]{2,1,0:T(2,128)(2,1)} %copy-done.12, f32[1,2048]{1,0:T(1,128)} %bitcast.78, bf16[2,128,2048]{2,1,0:T(8,128)(2,1)} %embedded.1, f32[1,2048]{1,0:T(1,128)} %bitcast.79, bf16[4096,512]{1,0:T(8,128)(2,1)} %projection.1), custom_call_target="tpu_custom_call" | custom-call | flops 1073741824 | bytes 4194304 | tf_op jit(solution)/shard_map/mix/pallas_call | solution.py:333
  13.6 1.6 collective-permute-start.3
  15.2 6.6 %collective-permute-done.3.above = bf16[256,512]{1,0:T(8,128)(2,1)} collective-permute-done((bf16[256,512]{1,0:T(8,128)(2,1)}, bf16[256,512]{1,0:T(8,128)(2,1)}, u32[]{:S(2)}, u32[]{:S(2)}) %collective-permute-start.3) | collective-permute-done | bytes 262176 | tf_op jit(solution)/shard_map/ppermute | solution.py:421
  21.8 0.1 stack.43.scalars.refs_0_
  21.9 1.8 %collective-permute-done.4.across = bf16[256,512]{1,0:T(8,128)(2,1)} collective-permute-done((bf16[256,512]{1,0:T(8,128)(2,1)}, bf16[256,512]{1,0:T(8,128)(2,1)}, u32[]{:S(2)}, u32[]{:S(2)}) %collective-permute-start.4) | collective-permute-done | bytes 262176 | tf_op jit(solution)/shard_map/ppermute | solution.py:421
  23.6 0.9 copy-done.4
  24.6 1.8 %arrange.1.refs_7_ = bf16[256,2048]{1,0:T(8,128)(2,1)S(1)} custom-call(s32[7]{0:T(128)S(1)} %stack.43.scalars.refs_0_, bf16[256,512]{1,0:T(8,128)(2,1)S(1)} %copy-done.4, bf16[256,512]{1,0:T(8,128)(2,1)} %collective-permute-done.2.beside, bf16[256,512]{1,0:T(8,128)(2,1)} %collective-permute-done.3.above, bf16[256,512]{1,0:T(8,128)(2,1)} %collective-permute-done.4.across, ...), custom_call_target="tpu_custom_call" | custom-call | flops 2097152 | bytes 2097152 | tf_op jit(solution)/shard_map/arrange/pallas_call | solution.py:368
  26.4 2.1 %collective-permute-start.5 = (bf16[256,2048]{1,0:T(8,128)(2,1)S(1)}, bf16[256,2048]{1,0:T(8,128)(2,1)}, u32[]{:S(2)}, u32[]{:S(2)}) collective-permute-start(bf16[256,2048]{1,0:T(8,128)(2,1)S(1)} %arrange.1.refs_7_), channel_id=1, source_target_pairs={{0,4},{1,9},{2,6},{3,11},{4,12},{5,1},{6,14},{7,3},{8,0},{9,17},{1... | collective-permute-start | bytes 3145736 | tf_op jit(solution)/shard_map/ppermute | solution.py:462
  28.4 1.0 copy-done.1
  29.4 12.9 %collective-permute-done.5.refs_5_ = bf16[256,2048]{1,0:T(8,128)(2,1)} collective-permute-done((bf16[256,2048]{1,0:T(8,128)(2,1)S(1)}, bf16[256,2048]{1,0:T(8,128)(2,1)}, u32[]{:S(2)}, u32[]{:S(2)}) %collective-permute-start.5) | collective-permute-done | bytes 1048608 | tf_op jit(solution)/shard_map/ppermute | solution.py:462
  42.3 1.0 collective-permute-start.8
  43.4 2.8 %main_rows.1.refs_6_ = bf16[136,2048]{1,0:T(8,128)(2,1)} custom-call(s32[7]{0:T(128)} %copy-done.5, s32[2]{0:T(128)} %lengths.1, bf16[2,128,2048]{2,1,0:T(8,128)(2,1)} %hidden.5, f32[1,2048]{1,0:T(1,128)} %bitcast.58, s32[2,128]{1,0:T(2,128)} %targets.1, s32[2,128]{1,0:T(2,128)} %main_mask.1, s32[2,128]{1,0:T(2,128)} %mtp_mask.1), custom_call_target="tpu_custom_call" | custom-call | flops 1048576 | bytes 524288 | tf_op jit(solution)/shard_map/main_rows/pallas_call | solution.py:231
  46.2 1.6 collective-permute-start.6
  47.8 15.5 %collective-permute-done.6.refs_6_.refs_5_ = bf16[136,2048]{1,0:T(8,128)(2,1)S(1)} collective-permute-done((bf16[136,2048]{1,0:T(8,128)(2,1)}, bf16[136,2048]{1,0:T(8,128)(2,1)S(1)}, u32[]{:S(2)}, u32[]{:S(2)}) %collective-permute-start.6) | collective-permute-done | bytes 557088 | tf_op jit(solution)/shard_map/ppermute | solution.py:462
  63.3 1.0 collective-permute-start.9
  64.3 1.6 collective-permute-start.11
  65.9 6.9 %collective-permute-done.9.refs_6_.refs_5_ = bf16[136,2048]{1,0:T(8,128)(2,1)S(1)} collective-permute-done((bf16[136,2048]{1,0:T(8,128)(2,1)S(1)}, bf16[136,2048]{1,0:T(8,128)(2,1)S(1)}, u32[]{:S(2)}, u32[]{:S(2)}) %collective-permute-start.9) | collective-permute-done | bytes 557088 | tf_op jit(solution)/shard_map/ppermute | solution.py:462
  72.8 1.0 collective-permute-start.12
  73.9 16.2 %collective-permute-done.12.refs_6_.refs_5_.block = bf16[136,2048]{1,0:T(8,128)(2,1)S(1)} collective-permute-done((bf16[136,2048]{1,0:T(8,128)(2,1)S(1)}, bf16[136,2048]{1,0:T(8,128)(2,1)S(1)}, u32[]{:S(2)}, u32[]{:S(2)}) %collective-permute-start.12) | collective-permute-done | bytes 557088 | tf_op jit(solution)/shard_map/ppermute | solution.py:462
  90.0 0.7 copy-done.6
  90.7 0.6 half.2
  91.3 1.1 collective-permute-start.14
  92.4 0.7 copy-done.7
  93.0 0.8 mine.1.refs_5_
  93.8 1.6 collective-permute-start.7
  95.4 0.5 collective-permute-start.10
  95.9 2.2 %collective-permute-done.14.refs_5_ = bf16[72,2048]{1,0:T(8,128)(2,1)S(1)} collective-permute-done((bf16[72,2048]{1,0:T(8,128)(2,1)S(1)}, bf16[72,2048]{1,0:T(8,128)(2,1)S(1)}, u32[]{:S(2)}, u32[]{:S(2)}) %collective-permute-start.14) | collective-permute-done | bytes 294944 | tf_op jit(solution)/shard_map/ppermute | solution.py:462
  98.0 1.5 collective-permute-start.13
  99.6 0.5 collective-permute-start.15
  100.1 0.6 half.3
  100.7 1.3 collective-permute-start.16
  102.0 1.2 copy-done.2
  103.2 1.1 copy-done.3
  104.2 0.7 copy-done.8
  104.9 5.8 %shard_map.139 = (f32[4,32,128]{2,1,0:T(8,128)S(1)}, f32[32,128]{1,0:T(8,128)S(1)}, bf16[1600,2048]{1,0:T(8,128)(2,1)S(1)}) custom-call(s32[7]{0:T(128)S(1)} %copy-done.8, f32[4,32,128]{2,1,0:T(8,128)S(1)} %copy-done.9, f32[32,128]{1,0:T(8,128)S(1)} %broadcast_in_dim.3.refs_2_, bf16[1600,2048]{1,0:T(8,128)(2,1)S(1)} %bitcast.50, ...), custom_call_target="tpu_custom_call" | custom-call | flops 3355443200 | bytes 14155776 | tf_op jit(solution)/shard_map/pallas_call | solution.py:174
  110.6 5.5 %shard_map.140 = (f32[4,32,128]{2,1,0:T(8,128)S(1)}, f32[32,128]{1,0:T(8,128)S(1)}) custom-call(s32[7]{0:T(128)S(1)} %copy-done.8, f32[4,32,128]{2,1,0:T(8,128)S(1)} %get-tuple-element.19.refs_1_, f32[32,128]{1,0:T(8,128)S(1)} %get-tuple-element.20.refs_2_, bf16[1600,2048]{1,0:T(8,128)(2,1)S(1)} %bitcast.51, ...), custom_call_target="tpu_custom_call" | custom-call | flops 3355443200 | bytes 14155776 | tf_op jit(solution)/shard_map/pallas_call | solution.py:174
  116.1 4.8 %shard_map.141 = (f32[4,32,128]{2,1,0:T(8,128)S(1)}, f32[32,128]{1,0:T(8,128)S(1)}) custom-call(s32[7]{0:T(128)S(1)} %copy-done.8, f32[4,32,128]{2,1,0:T(8,128)S(1)} %get-tuple-element.22.refs_1_, f32[32,128]{1,0:T(8,128)S(1)} %get-tuple-element.23.refs_2_, bf16[1600,2048]{1,0:T(8,128)(2,1)S(1)} %bitcast.52, ...), custom_call_target="tpu_custom_call" | custom-call | flops 3355443200 | bytes 14155776 | tf_op jit(solution)/shard_map/pallas_call | solution.py:174
  121.0 5.7 %shard_map.142 = (f32[4,32,128]{2,1,0:T(8,128)S(1)}, f32[32,128]{1,0:T(8,128)S(1)}) custom-call(s32[7]{0:T(128)S(1)} %copy-done.8, f32[4,32,128]{2,1,0:T(8,128)S(1)} %get-tuple-element.24.refs_1_, f32[32,128]{1,0:T(8,128)S(1)} %get-tuple-element.25.refs_2_, bf16[1600,2048]{1,0:T(8,128)(2,1)S(1)} %bitcast.53, ...), custom_call_target="tpu_custom_call" | custom-call | flops 3355443200 | bytes 14155776 | tf_op jit(solution)/shard_map/pallas_call | solution.py:174
  126.7 4.8 %shard_map.143 = (f32[4,32,128]{2,1,0:T(8,128)S(1)}, f32[32,128]{1,0:T(8,128)S(1)}) custom-call(s32[7]{0:T(128)S(1)} %copy-done.8, f32[4,32,128]{2,1,0:T(8,128)S(1)} %get-tuple-element.26.refs_1_, f32[32,128]{1,0:T(8,128)S(1)} %get-tuple-element.27.refs_2_, bf16[1600,2048]{1,0:T(8,128)(2,1)S(1)} %bitcast.54, ...), custom_call_target="tpu_custom_call" | custom-call | flops 3355443200 | bytes 14155776 | tf_op jit(solution)/shard_map/pallas_call | solution.py:174
  131.5 4.8 %shard_map.144 = (f32[4,32,128]{2,1,0:T(8,128)S(1)}, f32[32,128]{1,0:T(8,128)S(1)}) custom-call(s32[7]{0:T(128)S(1)} %copy-done.8, f32[4,32,128]{2,1,0:T(8,128)S(1)} %get-tuple-element.28.refs_1_, f32[32,128]{1,0:T(8,128)S(1)} %get-tuple-element.29.refs_2_, bf16[1600,2048]{1,0:T(8,128)(2,1)S(1)} %bitcast.55, ...), custom_call_target="tpu_custom_call" | custom-call | flops 3355443200 | bytes 14155776 | tf_op jit(solution)/shard_map/pallas_call | solution.py:174
  136.3 4.8 %shard_map.145 = (f32[4,32,128]{2,1,0:T(8,128)S(1)}, f32[32,128]{1,0:T(8,128)S(1)}) custom-call(s32[7]{0:T(128)S(1)} %copy-done.8, f32[4,32,128]{2,1,0:T(8,128)S(1)} %get-tuple-element.30.refs_1_, f32[32,128]{1,0:T(8,128)S(1)} %get-tuple-element.31.refs_2_, bf16[1600,2048]{1,0:T(8,128)(2,1)S(1)} %bitcast.56, ...), custom_call_target="tpu_custom_call" | custom-call | flops 3355443200 | bytes 14155776 | tf_op jit(solution)/shard_map/pallas_call | solution.py:174
  141.1 5.3 %shard_map.146 = (f32[4,32,128]{2,1,0:T(8,128)S(1)}, f32[32,128]{1,0:T(8,128)}) custom-call(s32[7]{0:T(128)S(1)} %copy-done.8, f32[4,32,128]{2,1,0:T(8,128)S(1)} %get-tuple-element.32.refs_1_, f32[32,128]{1,0:T(8,128)S(1)} %get-tuple-element.33.refs_2_, bf16[1600,2048]{1,0:T(8,128)(2,1)S(1)} %bitcast.57, bf16[1600,2048]{1,0:T(8,128)(2,1)S(1)} %get-tuple-element.21.refs_4_, ...), custom_call_target="tpu_custom_call" | custom-call | flops 3355443200 | bytes 14155776 | tf_op jit(solution)/shard_map/pallas_call | solution.py:174
  146.5 1.3 collective-permute-done.17
  147.8 2.6 %collective-permute-start.18 = (f32[3,32,128]{2,1,0:T(8,128)S(1)}, f32[3,32,128]{2,1,0:T(8,128)S(1)}, u32[]{:S(2)}, u32[]{:S(2)}) collective-permute-start(f32[3,32,128]{2,1,0:T(8,128)S(1)} %pad_maximum_fusion), channel_id=1, source_target_pairs={{0,6},{1,7},{2,4},{3,5},{4,2},{5,3},{6,0},{7,1},{8,14},{9,15},{10,... | collective-permute-start | bytes 147464 | tf_op jit(solution)/shard_map/ppermute | solution.py:569
  150.4 0.4 collective-permute-start.19
  150.8 0.5 collective-permute-start.20
  151.3 1.5 collective-permute-done.18
  152.9 1.6 collective-permute-done.19
  154.5 0.4 collective-permute-done.20
  155.0 3.5 %collective-permute-start.21 = (f32[3,32,128]{2,1,0:T(8,128)S(1)}, f32[3,32,128]{2,1,0:T(8,128)S(1)}, u32[]{:S(2)}, u32[]{:S(2)}) collective-permute-start(f32[3,32,128]{2,1,0:T(8,128)S(1)} %pad_maximum_fusion.1), channel_id=1, source_target_pairs={{0,24},{1,25},{2,26},{3,27},{4,28},{5,29},{6,30},{7,31},{8,16},{9,... | collective-permute-start | bytes 147464 | tf_op jit(solution)/shard_map/ppermute | solution.py:569
  158.5 0.9 collective-permute-start.23
  159.5 1.6 collective-permute-done.21
  161.1 2.4 %collective-permute-done.22 = f32[3,32,128]{2,1,0:T(8,128)S(1)} collective-permute-done((f32[3,32,128]{2,1,0:T(8,128)S(1)}, f32[3,32,128]{2,1,0:T(8,128)S(1)}, u32[]{:S(2)}, u32[]{:S(2)}) %collective-permute-start.22) | collective-permute-done | bytes 49184 | tf_op jit(solution)/shard_map/ppermute | solution.py:569
  163.6 0.1 fusion.17
  163.8 0.1 reduce_sum.37
  163.9 0.1 reduce_sum.24
  164.0 0.1 reduce_sum.25
  164.2 0.6 slice_bitcast_fusion
  164.8 0.6 fusion.21
  (54 shorter events, 0.4 us)
Async XLA Ops:
  0.6 91.7 %copy-start = (bf16[2,128,2048]{2,1,0:T(8,128)(2,1)S(1)}, bf16[2,128,2048]{2,1,0:T(8,128)(2,1)}, u32[]{:S(2)}) copy-start(bf16[2,128,2048]{2,1,0:T(8,128)(2,1)} %hidden.5) | copy-start | bytes 3145732
  0.6 23.0 %copy-start.11 = (f32[2048]{0:T(1024)S(1)}, f32[2048]{0:T(1024)}, u32[]{:S(2)}) copy-start(f32[2048]{0:T(1024)} %param.23) | copy-start | bytes 24580
  0.7 91.7 %copy-start.10 = (f32[2048]{0:T(1024)S(1)}, f32[2048]{0:T(1024)}, u32[]{:S(2)}) copy-start(f32[2048]{0:T(1024)} %param.20) | copy-start | bytes 24580
  0.7 100.0 %collective-permute-start = (bf16[1600,2048]{1,0:T(8,128)(2,1)}, bf16[1600,2048]{1,0:T(8,128)(2,1)}, u32[]{:S(2)}, u32[]{:S(2)}) collective-permute-start(bf16[1600,2048]{1,0:T(8,128)(2,1)} %bitcast.47), channel_id=1, source_target_pairs={{0,1},{1,0},{2,3},{3,2},{4,5},{5,4},{6,7},{7,6},{8,9},{9,8},{10,11... | collective-permute-start | bytes 19660808 | tf_op jit(solution)/shard_map/ppermute | solution.py:421
  2.1 5.9 %collective-permute-start.1 = (bf16[2,1,2048]{2,1,0:T(2,128)(2,1)S(1)}, bf16[2,1,2048]{2,1,0:T(2,128)(2,1)S(1)}, u32[]{:S(2)}, u32[]{:S(2)}) collective-permute-start(bf16[2,1,2048]{2,1,0:T(2,128)(2,1)S(1)} %slice.129), channel_id=1, source_target_pairs={{0,4},{4,8},{8,12},{12,16},{16,20},{20,24},{24,28},{1,5},{5,9},{9,... | collective-permute-start | bytes 24584 | tf_op jit(solution)/shard_map/ppermute | solution.py:429
  8.0 0.6 copy-start.12
  8.6 93.4 %slice-start = ((s8[6553600]{0:T(1024)(128)(4,1)}), s8[2359296]{0:T(1024)(128)(4,1)S(1)}, s32[]{:S(2)}) async-start(s8[6553600]{0:T(1024)(128)(4,1)} %bitcast.48), calls=%async_computation | async-start | bytes 4718592
  8.6 93.4 %copy-start.9 = (f32[4,32,128]{2,1,0:T(8,128)S(1)}, f32[4,32,128]{2,1,0:T(8,128)}, u32[]{:S(2)}) copy-start(f32[4,32,128]{2,1,0:T(8,128)} %constant.40.clone.1.refs_1_) | copy-start | bytes 196612
  13.6 8.2 %collective-permute-start.3 = (bf16[256,512]{1,0:T(8,128)(2,1)}, bf16[256,512]{1,0:T(8,128)(2,1)}, u32[]{:S(2)}, u32[]{:S(2)}) collective-permute-start(bf16[256,512]{1,0:T(8,128)(2,1)} %mix.1.mine), channel_id=1, source_target_pairs={{0,2},{1,3},{2,0},{3,1},{4,6},{5,7},{6,4},{7,5},{8,10},{9,11},{10,... | collective-permute-start | bytes 786440 | tf_op jit(solution)/shard_map/ppermute | solution.py:421
  15.2 6.7 %collective-permute-start.2 = (bf16[256,512]{1,0:T(8,128)(2,1)}, bf16[256,512]{1,0:T(8,128)(2,1)}, u32[]{:S(2)}, u32[]{:S(2)}) collective-permute-start(bf16[256,512]{1,0:T(8,128)(2,1)} %mix.1.mine), channel_id=1, source_target_pairs={{0,1},{1,0},{2,3},{3,2},{4,5},{5,4},{6,7},{7,6},{8,9},{9,8},{10,11... | collective-permute-start | bytes 786440 | tf_op jit(solution)/shard_map/ppermute | solution.py:421
  21.8 1.9 %collective-permute-start.4 = (bf16[256,512]{1,0:T(8,128)(2,1)}, bf16[256,512]{1,0:T(8,128)(2,1)}, u32[]{:S(2)}, u32[]{:S(2)}) collective-permute-start(bf16[256,512]{1,0:T(8,128)(2,1)} %collective-permute-done.3.above), channel_id=1, source_target_pairs={{0,1},{1,0},{2,3},{3,2},{4,5},{5,4},{6,7},{7,6},{8,9},{9,8},{10,11... | collective-permute-start | bytes 786440 | tf_op jit(solution)/shard_map/ppermute | solution.py:421
  21.8 21.5 %copy-start.5 = (s32[7]{0:T(128)}, s32[7]{0:T(128)S(1)}, u32[]{:S(2)}) copy-start(s32[7]{0:T(128)S(1)} %stack.43.scalars.refs_0_) | copy-start | bytes 88
  23.6 1.0 copy-start.4
  24.6 77.3 %slice-start.1 = ((s8[6553600]{0:T(1024)(128)(4,1)}), s8[4194304]{0:T(1024)(128)(4,1)S(1)}, s32[]{:S(2)}) async-start(s8[6553600]{0:T(1024)(128)(4,1)} %bitcast.48), calls=%async_computation.1 | async-start | bytes 8388608
  26.4 15.9 %collective-permute-start.5 = (bf16[256,2048]{1,0:T(8,128)(2,1)S(1)}, bf16[256,2048]{1,0:T(8,128)(2,1)}, u32[]{:S(2)}, u32[]{:S(2)}) collective-permute-start(bf16[256,2048]{1,0:T(8,128)(2,1)S(1)} %arrange.1.refs_7_), channel_id=1, source_target_pairs={{0,4},{1,9},{2,6},{3,11},{4,12},{5,1},{6,14},{7,3},{8,0},{9,17},{1... | collective-permute-start | bytes 3145736 | tf_op jit(solution)/shard_map/ppermute | solution.py:462
  28.4 1.0 copy-start.1
  42.3 22.0 %collective-permute-start.8 = (bf16[256,2048]{1,0:T(8,128)(2,1)}, bf16[256,2048]{1,0:T(8,128)(2,1)}, u32[]{:S(2)}, u32[]{:S(2)}) collective-permute-start(bf16[256,2048]{1,0:T(8,128)(2,1)} %collective-permute-done.5.refs_5_), channel_id=1, source_target_pairs={{0,4},{1,9},{2,6},{3,11},{4,12},{5,1},{6,14},{7,3},{8,0},{9,17},{1... | collective-permute-start | bytes 3145736 | tf_op jit(solution)/shard_map/ppermute | solution.py:462
  46.2 17.1 %collective-permute-start.6 = (bf16[136,2048]{1,0:T(8,128)(2,1)}, bf16[136,2048]{1,0:T(8,128)(2,1)S(1)}, u32[]{:S(2)}, u32[]{:S(2)}) collective-permute-start(bf16[136,2048]{1,0:T(8,128)(2,1)} %main_rows.1.refs_6_), channel_id=1, source_target_pairs={{0,4},{1,9},{2,6},{3,11},{4,12},{5,1},{6,14},{7,3},{8,0},{9,17},{1... | collective-permute-start | bytes 1671176 | tf_op jit(solution)/shard_map/ppermute | solution.py:462
  63.3 9.5 %collective-permute-start.9 = (bf16[136,2048]{1,0:T(8,128)(2,1)S(1)}, bf16[136,2048]{1,0:T(8,128)(2,1)S(1)}, u32[]{:S(2)}, u32[]{:S(2)}) collective-permute-start(bf16[136,2048]{1,0:T(8,128)(2,1)S(1)} %collective-permute-done.6.refs_6_.refs_5_), channel_id=1, source_target_pairs={{0,4},{1,9},{2,6},{3,11},{4,12},{5,1},{6,14},{7,3},{8,0},{9,17},{1... | collective-permute-start | bytes 1671176 | tf_op jit(solution)/shard_map/ppermute | solution.py:462
  64.3 35.2 %collective-permute-start.11 = (bf16[256,2048]{1,0:T(8,128)(2,1)}, bf16[256,2048]{1,0:T(8,128)(2,1)S(1)}, u32[]{:S(2)}, u32[]{:S(2)}) collective-permute-start(bf16[256,2048]{1,0:T(8,128)(2,1)} %collective-permute-done.8.refs_5_), channel_id=1, source_target_pairs={{0,4},{1,9},{2,6},{3,11},{4,12},{5,1},{6,14},{7,3},{8,0},{9,17},{1... | collective-permute-start | bytes 3145736 | tf_op jit(solution)/shard_map/ppermute | solution.py:462
  72.8 17.2 %collective-permute-start.12 = (bf16[136,2048]{1,0:T(8,128)(2,1)S(1)}, bf16[136,2048]{1,0:T(8,128)(2,1)S(1)}, u32[]{:S(2)}, u32[]{:S(2)}) collective-permute-start(bf16[136,2048]{1,0:T(8,128)(2,1)S(1)} %collective-permute-done.9.refs_6_.refs_5_), channel_id=1, source_target_pairs={{0,4},{1,9},{2,6},{3,11},{4,12},{5,1},{6,14},{7,3},{8,0},{9,17},{1... | collective-permute-start | bytes 1671176 | tf_op jit(solution)/shard_map/ppermute | solution.py:462
  90.0 0.7 copy-start.6
  91.3 6.8 %collective-permute-start.14 = (bf16[72,2048]{1,0:T(8,128)(2,1)S(1)}, bf16[72,2048]{1,0:T(8,128)(2,1)S(1)}, u32[]{:S(2)}, u32[]{:S(2)}) collective-permute-start(bf16[72,2048]{1,0:T(8,128)(2,1)S(1)} %half.2), channel_id=1, source_target_pairs={{0,4},{1,9},{2,6},{3,11},{4,12},{5,1},{6,14},{7,3},{8,0},{9,17},{1... | collective-permute-start | bytes 884744 | tf_op jit(solution)/shard_map/ppermute | solution.py:462
  92.3 0.7 copy-start.7
  93.8 22.3 %collective-permute-start.7 = (bf16[136,2048]{1,0:T(8,128)(2,1)S(1)}, bf16[136,2048]{1,0:T(8,128)(2,1)S(1)}, u32[]{:S(2)}, u32[]{:S(2)}) collective-permute-start(bf16[136,2048]{1,0:T(8,128)(2,1)S(1)} %collective-permute-done.6.refs_6_.refs_5_), channel_id=1, source_target_pairs={{0,2},{1,3},{2,0},{3,1},{4,6},{5,7},{6,4},{7,5},{8,10},{9,11},{10,... | collective-permute-start | bytes 1671176 | tf_op jit(solution)/shard_map/ppermute | solution.py:421
  95.4 31.3 %collective-permute-start.10 = (bf16[136,2048]{1,0:T(8,128)(2,1)S(1)}, bf16[136,2048]{1,0:T(8,128)(2,1)S(1)}, u32[]{:S(2)}, u32[]{:S(2)}) collective-permute-start(bf16[136,2048]{1,0:T(8,128)(2,1)S(1)} %collective-permute-done.9.refs_6_.refs_5_), channel_id=1, source_target_pairs={{0,2},{1,3},{2,0},{3,1},{4,6},{5,7},{6,4},{7,5},{8,10},{9,11},{10,... | collective-permute-start | bytes 1671176 | tf_op jit(solution)/shard_map/ppermute | solution.py:421
  98.0 38.2 %collective-permute-start.13 = (bf16[136,2048]{1,0:T(8,128)(2,1)S(1)}, bf16[136,2048]{1,0:T(8,128)(2,1)S(1)}, u32[]{:S(2)}, u32[]{:S(2)}) collective-permute-start(bf16[136,2048]{1,0:T(8,128)(2,1)S(1)} %collective-permute-done.12.refs_6_.refs_5_.block), channel_id=1, source_target_pairs={{0,2},{1,3},{2,0},{3,1},{4,6},{5,7},{6,4},{7,5},{8,10},{9,11},{10,... | collective-permute-start | bytes 1671176 | tf_op jit(solution)/shard_map/ppermute | solution.py:421
  99.6 41.6 %collective-permute-start.15 = (bf16[72,2048]{1,0:T(8,128)(2,1)S(1)}, bf16[72,2048]{1,0:T(8,128)(2,1)S(1)}, u32[]{:S(2)}, u32[]{:S(2)}) collective-permute-start(bf16[72,2048]{1,0:T(8,128)(2,1)S(1)} %collective-permute-done.14.refs_5_), channel_id=1, source_target_pairs={{0,2},{1,3},{2,0},{3,1},{4,6},{5,7},{6,4},{7,5},{8,10},{9,11},{10,... | collective-permute-start | bytes 884744 | tf_op jit(solution)/shard_map/ppermute | solution.py:421
  100.7 40.5 %collective-permute-start.16 = (bf16[128,2048]{1,0:T(8,128)(2,1)S(1)}, bf16[128,2048]{1,0:T(8,128)(2,1)S(1)}, u32[]{:S(2)}, u32[]{:S(2)}) collective-permute-start(bf16[128,2048]{1,0:T(8,128)(2,1)S(1)} %half.3), channel_id=1, source_target_pairs={{0,4},{1,9},{2,6},{3,11},{4,12},{5,1},{6,14},{7,3},{8,0},{9,17},{1... | collective-permute-start | bytes 1572872 | tf_op jit(solution)/shard_map/ppermute | solution.py:462
  101.9 1.2 copy-start.2
  103.2 1.1 copy-start.3
  104.2 0.7 copy-start.8
  146.5 1.3 collective-permute-start.17
  147.8 5.1 %collective-permute-start.18 = (f32[3,32,128]{2,1,0:T(8,128)S(1)}, f32[3,32,128]{2,1,0:T(8,128)S(1)}, u32[]{:S(2)}, u32[]{:S(2)}) collective-permute-start(f32[3,32,128]{2,1,0:T(8,128)S(1)} %pad_maximum_fusion), channel_id=1, source_target_pairs={{0,6},{1,7},{2,4},{3,5},{4,2},{5,3},{6,0},{7,1},{8,14},{9,15},{10,... | collective-permute-start | bytes 147464 | tf_op jit(solution)/shard_map/ppermute | solution.py:569
  150.4 4.1 %collective-permute-start.19 = (f32[3,32,128]{2,1,0:T(8,128)S(1)}, f32[3,32,128]{2,1,0:T(8,128)S(1)}, u32[]{:S(2)}, u32[]{:S(2)}) collective-permute-start(f32[3,32,128]{2,1,0:T(8,128)S(1)} %pad_maximum_fusion), channel_id=1, source_target_pairs={{0,4},{1,5},{2,6},{3,7},{4,0},{5,1},{6,2},{7,3},{8,12},{9,13},{10,... | collective-permute-start | bytes 147464 | tf_op jit(solution)/shard_map/ppermute | solution.py:569
  150.8 4.1 %collective-permute-start.20 = (f32[3,32,128]{2,1,0:T(8,128)S(1)}, f32[3,32,128]{2,1,0:T(8,128)S(1)}, u32[]{:S(2)}, u32[]{:S(2)}) collective-permute-start(f32[3,32,128]{2,1,0:T(8,128)S(1)} %pad_maximum_fusion), channel_id=1, source_target_pairs={{0,2},{1,3},{2,0},{3,1},{4,6},{5,7},{6,4},{7,5},{8,10},{9,11},{10,... | collective-permute-start | bytes 147464 | tf_op jit(solution)/shard_map/ppermute | solution.py:569
  155.0 6.1 %collective-permute-start.21 = (f32[3,32,128]{2,1,0:T(8,128)S(1)}, f32[3,32,128]{2,1,0:T(8,128)S(1)}, u32[]{:S(2)}, u32[]{:S(2)}) collective-permute-start(f32[3,32,128]{2,1,0:T(8,128)S(1)} %pad_maximum_fusion.1), channel_id=1, source_target_pairs={{0,24},{1,25},{2,26},{3,27},{4,28},{5,29},{6,30},{7,31},{8,16},{9,... | collective-permute-start | bytes 147464 | tf_op jit(solution)/shard_map/ppermute | solution.py:569
  158.5 5.0 %collective-permute-start.22 = (f32[3,32,128]{2,1,0:T(8,128)S(1)}, f32[3,32,128]{2,1,0:T(8,128)S(1)}, u32[]{:S(2)}, u32[]{:S(2)}) collective-permute-start(f32[3,32,128]{2,1,0:T(8,128)S(1)} %pad_maximum_fusion.1), channel_id=1, source_target_pairs={{0,16},{1,17},{2,18},{3,19},{4,20},{5,21},{6,22},{7,23},{8,24},{9,... | collective-permute-start | bytes 147464 | tf_op jit(solution)/shard_map/ppermute | solution.py:569
  158.5 5.0 %collective-permute-start.23 = (f32[3,32,128]{2,1,0:T(8,128)S(1)}, f32[3,32,128]{2,1,0:T(8,128)S(1)}, u32[]{:S(2)}, u32[]{:S(2)}) collective-permute-start(f32[3,32,128]{2,1,0:T(8,128)S(1)} %pad_maximum_fusion.1), channel_id=1, source_target_pairs={{0,8},{1,9},{2,10},{3,11},{4,12},{5,13},{6,14},{7,15},{8,0},{9,1},... | collective-permute-start | bytes 147464 | tf_op jit(solution)/shard_map/ppermute | solution.py:569

commit v3 on v2

--- a/solution.py
+++ b/solution.py
@@ -93,8 +93,8 @@
             ids = fields[0:1] * 256.0 + fields[1:2]
             ids_out[slot, :] = ids
             ids_out[pl.ds(below, 1), :] = ids
-            state[3, slot, :] = fields[2:3]
-            state[3, pl.ds(below, 1), :] = fields[3:4]
+            state[2, slot, :] = fields[2:3]
+            state[2, pl.ds(below, 1), :] = fields[3:4]
         ids = ids_out[slot, :].astype(jnp.int32)
         ids = jnp.broadcast_to(ids, (8, span)) - lax.broadcasted_iota(jnp.int32, (8, span), 0)
         wanted[:, at * span : (at + 1) * span] = ids
@@ -112,16 +112,16 @@
         new = jnp.maximum(old, jnp.max(logits, axis=0))
         top[...] = new
         offset = wanted[...] - (base + start)
-        fresh = total[...] * jnp.exp(old - new)
-        chosen = picked[...]
+        fresh = [total[...] * jnp.exp(old - new)] + [jnp.zeros(old.shape, jnp.float32)] * 3
+        chosen = [picked[...]] + [jnp.zeros(old.shape, jnp.float32)] * 3
         for i in range(tile // 8):
-            fresh += jnp.exp(logits[i] - new)
+            fresh[i % 4] += jnp.exp(logits[i] - new)
             reached = offset == 8 * i
             if valid < cols:
                 reached &= logits[i] > LOWEST
-            chosen = jnp.where(reached, logits[i], chosen)
-        total[...] = fresh
-        picked[...] = chosen
+            chosen[i % 4] = jnp.where(reached, logits[i], chosen[i % 4])
+        total[...] = (fresh[0] + fresh[1]) + (fresh[2] + fresh[3])
+        picked[...] = (chosen[0] + chosen[1]) + (chosen[2] + chosen[3])
 
     waiting = None
     at = 0
@@ -144,13 +144,13 @@
     fold(*waiting)
     highest = jnp.max(top[...], axis=0, keepdims=True)
     sums = jnp.sum(total[...] * jnp.exp(top[...] - highest), axis=0, keepdims=True)
+    weight = highest + jnp.log(sums)
     chosen = jnp.sum(picked[...], axis=0, keepdims=True)
     for at, (head, distance, batch, _, _) in enumerate(segments):
         lanes = slice(at * span, (at + 1) * span)
         slot = pl.ds(slot_of(head, distance, batch), 1)
-        state[0, slot, :] = highest[:, lanes]
-        state[1, slot, :] = sums[:, lanes]
-        state[2, slot, :] = chosen[:, lanes]
+        state[0, slot, :] = weight[:, lanes]
+        state[1, slot, :] = chosen[:, lanes]
 
 
 def head_stats(scalars, state, own, peer, valid, sources, segments, fetch):
@@ -249,24 +249,27 @@
     )(scalars, lengths, hidden, gain, targets, main_mask, mtp_mask)
 
 
-def mine_kernel(scalars, hidden, gain, mine):
-    mine[...] = normal_rows(hidden[scalars[6]], gain[...])
-
-
-def main_rows_mine(scalars, hidden, gain):
+def mine_kernel(scalars, hidden, gain, block, value, mine, held):
+    held[...] = value[...]
+    span = hidden.shape[1]
+    mine[:span, :] = normal_rows(hidden[scalars[6]], gain[...])
+    mine[span:, :] = block[block.shape[0] - META_ROWS :, :]
+
+
+def main_rows_mine(scalars, hidden, gain, block, value):
     vmem = pl.BlockSpec(memory_space=pltpu.VMEM)
-    shape = hidden.shape[1:]
+    shape = (hidden.shape[1] + META_ROWS, hidden.shape[2])
     return pl.pallas_call(
         mine_kernel,
-        in_specs=[pl.BlockSpec(memory_space=pltpu.SMEM), vmem, vmem],
-        out_specs=vmem,
-        out_shape=jax.ShapeDtypeStruct(shape, jnp.bfloat16),
+        in_specs=[pl.BlockSpec(memory_space=pltpu.SMEM), vmem, vmem, vmem, vmem],
+        out_specs=[vmem, vmem],
+        out_shape=[jax.ShapeDtypeStruct(s, jnp.bfloat16) for s in (shape, value.shape)],
         compiler_params=pltpu.CompilerParams(vmem_limit_bytes=VMEM_LIMIT),
         cost_estimate=pl.CostEstimate(
             flops=2 * shape[0] * shape[1], bytes_accessed=hidden.size, transcendentals=0
         ),
         name="mine",
-    )(scalars, hidden, gain)
+    )(scalars, hidden, gain, block, value)
 
 
 def half_kernel(share, below, scalars, block, half):
@@ -378,11 +381,56 @@
     )(scalars, *quarters, gain)
 
 
-def join_stats(earlier, latter):
-    highest = jnp.maximum(earlier[0], latter[0])
-    exp_total = earlier[1] * jnp.exp(earlier[0] - highest)
-    exp_total += latter[1] * jnp.exp(latter[0] - highest)
-    return jnp.stack([highest, exp_total, earlier[2] + latter[2]])
+def join_stats(parts):
+    highest = functools.reduce(jnp.maximum, [p[0] for p in parts])
+    total = sum(jnp.exp(p[0] - highest) for p in parts)
+    return jnp.stack([highest + jnp.log(total), sum(p[1] for p in parts)])
+
+
+def last_kernel(scalars, own, near, far_low, far_high, keep, main, mtp, total, tokens):
+    low, high = scalars[7] != 0, scalars[8] != 0
+    here = ordered(low, own[...], near[...])
+    there = ordered(low, far_low[...], far_high[...])
+    first = ordered(high, here[0], there[0])
+    second = ordered(high, here[1], there[1])
+    parts = [first[0], second[0], first[1], second[1]]
+    highest = functools.reduce(jnp.maximum, [p[0] for p in parts])
+    weight = highest + jnp.log(sum(jnp.exp(p[0] - highest) for p in parts))
+    losses = weight - sum(p[1] for p in parts)
+    tokens[...] = keep[...] * losses
+    half = tokens.shape[0] // 2
+    batches = main.shape[0]
+    main[...] = tokens[pl.ds(scalars[3] * batches, batches), :]
+    mtp[...] = tokens[pl.ds(half + scalars[3] * batches, batches), :]
+
+    def summed(values):
+        return jnp.sum(jnp.sum(values, axis=0, keepdims=True), axis=1, keepdims=True)
+
+    means = [
+        summed(tokens[at : at + half, :]) / jnp.maximum(summed(keep[at : at + half, :]), 1.0)
+        for at in (0, half)
+    ]
+    total[...] = means[0] + MTP_WEIGHT * means[1]
+
+
+def last_step(scalars, parts, keep, batches):
+    slots, seq_len = keep.shape
+    vmem = pl.BlockSpec(memory_space=pltpu.VMEM)
+    shapes = [(batches, seq_len), (batches, seq_len), (1, 1)]
+    return pl.pallas_call(
+        last_kernel,
+        in_specs=[pl.BlockSpec(memory_space=pltpu.SMEM)] + [vmem] * 5,
+        out_specs=[vmem] * 3,
+        out_shape=[jax.ShapeDtypeStruct(s, jnp.float32) for s in shapes],
+        scratch_shapes=[pltpu.VMEM(keep.shape, jnp.float32)],
+        compiler_params=pltpu.CompilerParams(vmem_limit_bytes=VMEM_LIMIT),
+        cost_estimate=pl.CostEstimate(
+            flops=30 * slots * seq_len,
+            bytes_accessed=36 * slots * seq_len,
+            transcendentals=5 * slots * seq_len,
+        ),
+        name="last",
+    )(scalars, *parts, keep)
 
 
 def ordered(swap, mine, other):
@@ -433,15 +481,19 @@
         place = jnp.where(seq_index == s, i, place)
     base_own = (seq_index * vocab_count + vocab_index) * block_cols
     base_peer = (seq_index * vocab_count + (vocab_index ^ 1)) * block_cols
-    scalars = jnp.stack(
-        [base_own, base_peer, row, place, 1 - 2 * core, seq_index * seq_len, core]
-    )
+    bits = [("vocab", 2 << b) for b in range((vocab_count // 2).bit_length() - 1)]
+    bits += [("seq", 1 << b) for b in range(seq_count.bit_length() - 1)]
+
+    def bit_of(bit):
+        return (seq_index if bit[0] == "seq" else vocab_index) & bit[1]
+
+    scalars = [base_own, base_peer, row, place, 1 - 2 * core, seq_index * seq_len, core]
+    scalars = jnp.stack(scalars + [bit_of(bit) for bit in bits[-2:]])
 
     gain_row = main_gain.reshape(1, -1)
     main_block = main_rows_below(
         parts, scalars, lengths, hidden, gain_row, targets, main_mask, mtp_mask
     )
-    main_mine = main_rows_mine(scalars, hidden, gain_row)
 
     def flat(s, v):
         return s * vocab_count + v
@@ -477,10 +529,11 @@
         embed_gain.reshape(1, -1),
         projection,
     )
+    main_mine, partial_held = main_rows_mine(scalars, hidden, gain_row, main_block, partial_value)
     if parts > 1:
         beside = across(partial_value, 1)
         above = across(partial_value, 2)
-        quarters = (partial_value, beside, above, across(above, 1))
+        quarters = (partial_held, beside, above, across(above, 1))
         mtp_block = arranged(scalars, quarters, mtp_gain.reshape(1, -1))
     else:
         mixed = lax.all_gather(partial_value, "vocab", axis=1, tiled=True)
@@ -492,7 +545,7 @@
     mtp_hops = hops(mtp_block, mtp_half)
 
     slots = 4 * seq_count
-    empty = [LOWEST, 0.0, 0.0, 0.0]
+    empty = [LOWEST, 0.0, 0.0]
     state = [
         jnp.stack([jnp.full((slots, seq_len), e, jnp.float32) for e in empty]),
         jnp.zeros((slots, seq_len), jnp.float32),
@@ -541,21 +594,18 @@
         ]
 
     own_rows = [
-        (0, 0, None, (main_block, 2 * share), [(main_mine, 0, seq_len, 0)]),
+        (0, 0, None, (main_mine, seq_len), [(main_mine, 0, seq_len, 0)]),
         (1, 0, None, None, [(mtp_block, 0, seq_len, 3)]),
     ]
     state = run(state, own_rows, True)
     for at in range(1, far):
+        state = run(state, main_pair(at))
         state = run(state, mtp_pair(at))
-        state = run(state, main_pair(at))
     last_rows = [
         main_segment(far, None),
         (1, far, None, None, [(mtp_hops[far - 1], 0, seq_len, 0)]),
     ]
     stats, _ = run(state, last_rows)
-
-    bits = [("vocab", 2 << b) for b in range((vocab_count // 2).bit_length() - 1)]
-    bits += [("seq", 1 << b) for b in range(seq_count.bit_length() - 1)]
 
     def swapped(value, chosen):
         masks = {"seq": 0, "vocab": 0}
@@ -568,35 +618,26 @@
         ]
         return lax.ppermute(value, AXES, pairs)
 
-    def is_set(bit):
-        return (seq_index if bit[0] == "seq" else vocab_index) & bit[1] != 0
-
-    stats, others = ordered(core == 1, stats, swapped(stats, [("vocab", 1)]))
-    keeps = stats[3] + others[3]
-    stats = join_stats(stats, others)
-    for at in range(0, len(bits), 2):
-        low, high = bits[at], bits[at + 1] if at + 1 < len(bits) else None
-        near = swapped(stats, [low])
-        if high is None:
-            stats = join_stats(*ordered(is_set(low), stats, near))
-        else:
-            far_low, far_high = swapped(stats, [high]), swapped(stats, [low, high])
-            here = ordered(is_set(low), stats, near)
-            there = ordered(is_set(low), far_low, far_high)
-            (a, c), (b, d) = (
-                ordered(is_set(high), here[0], there[0]),
-                ordered(is_set(high), here[1], there[1]),
-            )
-            stats = join_stats(join_stats(a, b), join_stats(c, d))
-
-    losses = stats[0] + jnp.log(stats[1]) - stats[2]
-    tokens = (keeps * losses).reshape(2, seq_count, batches, seq_len)
-    keeps = keeps.reshape(2, seq_count, batches, seq_len)
-    shown = lax.dynamic_index_in_dim(tokens, place, axis=1, keepdims=False)
-    sums = jnp.sum(tokens, axis=(1, 2, 3))
-    counts = jnp.maximum(jnp.sum(keeps, axis=(1, 2, 3)), 1.0)
-    total_loss = sums[0] / counts[0] + MTP_WEIGHT * sums[1] / counts[1]
-    return (shown[0], shown[1], total_loss)
+    others = swapped(stats, [("vocab", 1)])
+    keeps = stats[2] + others[2]
+    stats = jnp.stack([jnp.maximum(stats[0], others[0]), stats[1] + others[1]])
+    groups = [bits[:1]] if len(bits) % 2 else []
+    groups += [bits[i : i + 2] for i in range(len(bits) % 2, len(bits), 2)]
+    for group in groups:
+        near = swapped(stats, group[:1])
+        if len(group) == 1:
+            stats = join_stats(ordered(bit_of(group[0]) != 0, stats, near))
+            continue
+        low, high = group
+        parts = [stats, near, swapped(stats, [high]), swapped(stats, group)]
+        if group is groups[-1]:
+            main_tokens, mtp_tokens, total = last_step(scalars, parts, keeps, batches)
+            return (main_tokens, mtp_tokens, total.reshape(()))
+        here = ordered(bit_of(low) != 0, stats, near)
+        there = ordered(bit_of(low) != 0, parts[2], parts[3])
+        first = ordered(bit_of(high) != 0, here[0], there[0])
+        second = ordered(bit_of(high) != 0, here[1], there[1])
+        stats = join_stats([first[0], second[0], first[1], second[1]])
 
 
 def solution(mesh):

time: 170 us -> 169 us (level)
  waiting for transfers between devices: 72.3 us -> 81.7 us
  local copies, waits for them, and re-layouts: 9.07 us -> 4.73 us
  between operations: 4.66 us -> 0.89 us
    ppermute x8, waiting for transfers between devices: 53.6 us -> 58.7 us  [hops(): block = lax.ppermute(block, AXES, onward)]
    unnamed x30 -> x22, local copies, waits for them, and re-layouts: 6.78 us -> 3.24 us
    ppermute x8, waiting for transfers between devices: 8.37 us -> 11.6 us  [across(): return lax.ppermute(value, 'vocab', pairs)]
    pallas_call x8, Pallas kernels: 41.5 us -> 38.8 us  [head_stats(): pl.pallas_call(functools.partial(head_kernel, segments, valid, len(source...]
  transfers between devices with their start and end apart: 24 -> 24, of which waited for: 14 -> 16; matrix products, arithmetic and copies ran while one was open for 1% -> 1% of each run, Pallas kernels for 28% -> 27%
where the time goes in v3:
time: 169 us
  waiting for transfers between devices  81.7 us (48%)
  Pallas kernels  51.9 us (31%)
  starting transfers between devices  29.4 us (17%)
  local copies, waits for them, and re-layouts  4.73 us (3%)
    ppermute x8, waiting for transfers between devices, hops(): block = lax.ppermute(block, AXES, onward)  58.7 us
    pallas_call x8, Pallas kernels, head_stats(): pl.pallas_call(functools.partial(head_kernel, segments, valid, len(source...  38.8 us
    ppermute x8, waiting for transfers between devices, across(): return lax.ppermute(value, 'vocab', pairs)  11.6 us
    ppermute x8, starting transfers between devices, hops(): block = lax.ppermute(block, AXES, onward)  10.7 us
    ppermute x7, waiting for transfers between devices, swapped(): return lax.ppermute(value, AXES, pairs)  9.96 us
    ppermute x7, starting transfers between devices, swapped(): return lax.ppermute(value, AXES, pairs)  8.08 us
    ppermute x8, starting transfers between devices, across(): return lax.ppermute(value, 'vocab', pairs)  6.2 us
    pallas_call x1, Pallas kernels, projected(): pl.pallas_call(mix_kernel, in_specs=[far] * len(operands), out_specs=pl.B...  5.02 us
  transfers between devices with their start and end apart: 24, of which 16 were waited for; matrix products, arithmetic and copies ran while one was open for 1% of the time, Pallas kernels for 27%

profile of v3, /device:TPU:0, one launch (start us, length us, event | category | flops | bytes accessed | tf_op | source)
XLA Modules:
  0.0 168.7 jit_solution(13358137849715926511)
XLA Ops:
  0.6 0.0 copy-start
  0.6 0.0 copy-start.6
  0.7 0.6 collective-permute-start
  1.2 0.9 slice.49
  2.1 4.5 %collective-permute-start.1 = (bf16[2,1,2048]{2,1,0:T(2,128)(2,1)S(1)}, bf16[2,1,2048]{2,1,0:T(2,128)(2,1)S(1)}, u32[]{:S(2)}, u32[]{:S(2)}) collective-permute-start(bf16[2,1,2048]{2,1,0:T(2,128)(2,1)S(1)} %slice.49), channel_id=1, source_target_pairs={{0,4},{4,8},{8,12},{12,16},{16,20},{20,24},{24,28},{1,5},{5,9},{9,... | collective-permute-start | bytes 24584 | tf_op jit(solution)/shard_map/ppermute | solution.py:477
  6.6 1.4 collective-permute-done.1.incoming
  8.0 0.6 copy-done.8
  8.6 5.0 %mix.1.value = bf16[256,512]{1,0:T(8,128)(2,1)} custom-call(bf16[2,128,2048]{2,1,0:T(8,128)(2,1)} %hidden.5, bf16[2,1,2048]{2,1,0:T(2,128)(2,1)} %copy-done.8, f32[1,2048]{1,0:T(1,128)} %bitcast.31, bf16[2,128,2048]{2,1,0:T(8,128)(2,1)} %embedded.1, f32[1,2048]{1,0:T(1,128)} %bitcast.32, bf16[4096,512]{1,0:T(8,128)(2,1)} %projection.1), custom_call_target="tpu_custom_call" | custom-call | flops 1073741824 | bytes 4194304 | tf_op jit(solution)/shard_map/mix/pallas_call | solution.py:336
  13.6 1.6 collective-permute-start.3
  15.2 0.0 collective-permute-start.2
  15.2 6.6 %collective-permute-done.3.above = bf16[256,512]{1,0:T(8,128)(2,1)} collective-permute-done((bf16[256,512]{1,0:T(8,128)(2,1)}, bf16[256,512]{1,0:T(8,128)(2,1)}, u32[]{:S(2)}, u32[]{:S(2)}) %collective-permute-start.3) | collective-permute-done | bytes 262176 | tf_op jit(solution)/shard_map/ppermute | solution.py:469
  21.8 0.0 collective-permute-start.4
  21.8 0.6 stack.49.scalars.refs_0_
  22.4 3.3 %main_rows.1.block = bf16[136,2048]{1,0:T(8,128)(2,1)} custom-call(s32[9]{0:T(128)} %stack.49.scalars.refs_0_, s32[2]{0:T(128)} %lengths.1, bf16[2,128,2048]{2,1,0:T(8,128)(2,1)} %hidden.5, f32[1,2048]{1,0:T(1,128)} %bitcast.28, s32[2,128]{1,0:T(2,128)} %targets.1, s32[2,128]{1,0:T(2,128)} %main_mask.1, s32[2,128]{1,0:T(2,128)} %mtp_mask.1), custom_call_target="tpu_custom_call" | custom-call | flops 1048576 | bytes 524288 | tf_op jit(solution)/shard_map/main_rows/pallas_call | solution.py:231
  25.8 1.0 copy-done.1
  26.8 0.9 copy-done.2
  27.8 0.6 copy-done.3
  28.4 0.8 mine.1
  29.2 0.0 collective-permute-done.2.beside
  29.2 1.6 arrange.1.refs_6_
  30.8 2.1 %collective-permute-start.7 = (bf16[256,2048]{1,0:T(8,128)(2,1)S(1)}, bf16[256,2048]{1,0:T(8,128)(2,1)S(1)}, u32[]{:S(2)}, u32[]{:S(2)}) collective-permute-start(bf16[256,2048]{1,0:T(8,128)(2,1)S(1)} %arrange.1.refs_6_), channel_id=1, source_target_pairs={{0,4},{1,9},{2,6},{3,11},{4,12},{5,1},{6,14},{7,3},{8,0},{9,17},{1... | collective-permute-start | bytes 3145736 | tf_op jit(solution)/shard_map/ppermute | solution.py:514
  32.9 13.8 %collective-permute-done.7.refs_5_ = bf16[256,2048]{1,0:T(8,128)(2,1)S(1)} collective-permute-done((bf16[256,2048]{1,0:T(8,128)(2,1)S(1)}, bf16[256,2048]{1,0:T(8,128)(2,1)S(1)}, u32[]{:S(2)}, u32[]{:S(2)}) %collective-permute-start.7) | collective-permute-done | bytes 1048608 | tf_op jit(solution)/shard_map/ppermute | solution.py:514
  46.7 1.0 collective-permute-start.10
  47.7 1.6 collective-permute-start.5
  49.3 18.2 %collective-permute-done.5.refs_5_.refs_6_ = bf16[136,2048]{1,0:T(8,128)(2,1)S(1)} collective-permute-done((bf16[136,2048]{1,0:T(8,128)(2,1)S(1)}, bf16[136,2048]{1,0:T(8,128)(2,1)S(1)}, u32[]{:S(2)}, u32[]{:S(2)}) %collective-permute-start.5) | collective-permute-done | bytes 557088 | tf_op jit(solution)/shard_map/ppermute | solution.py:514
  67.4 1.0 collective-permute-start.8
  68.5 1.6 collective-permute-start.13
  70.0 6.9 %collective-permute-done.8.refs_5_.refs_6_ = bf16[136,2048]{1,0:T(8,128)(2,1)S(1)} collective-permute-done((bf16[136,2048]{1,0:T(8,128)(2,1)S(1)}, bf16[136,2048]{1,0:T(8,128)(2,1)S(1)}, u32[]{:S(2)}, u32[]{:S(2)}) %collective-permute-start.8) | collective-permute-done | bytes 557088 | tf_op jit(solution)/shard_map/ppermute | solution.py:514
  77.0 1.0 collective-permute-start.11
  78.0 16.2 %collective-permute-done.11.refs_5_.refs_6_.block = bf16[136,2048]{1,0:T(8,128)(2,1)S(1)} collective-permute-done((bf16[136,2048]{1,0:T(8,128)(2,1)S(1)}, bf16[136,2048]{1,0:T(8,128)(2,1)S(1)}, u32[]{:S(2)}, u32[]{:S(2)}) %collective-permute-start.11) | collective-permute-done | bytes 557088 | tf_op jit(solution)/shard_map/ppermute | solution.py:514
  94.2 0.6 half.2
  94.7 1.1 collective-permute-start.14
  95.8 1.5 collective-permute-start.6
  97.3 0.5 collective-permute-start.9
  97.8 3.7 %collective-permute-done.14.refs_5_ = bf16[72,2048]{1,0:T(8,128)(2,1)S(1)} collective-permute-done((bf16[72,2048]{1,0:T(8,128)(2,1)S(1)}, bf16[72,2048]{1,0:T(8,128)(2,1)S(1)}, u32[]{:S(2)}, u32[]{:S(2)}) %collective-permute-start.14) | collective-permute-done | bytes 294944 | tf_op jit(solution)/shard_map/ppermute | solution.py:514
  101.5 1.5 collective-permute-start.12
  103.0 0.5 collective-permute-start.15
  103.5 0.6 half.3
  104.1 1.3 collective-permute-start.16
  105.4 5.7 %shard_map.139 = (f32[3,32,128]{2,1,0:T(8,128)S(1)}, f32[32,128]{1,0:T(8,128)S(1)}, bf16[1600,2048]{1,0:T(8,128)(2,1)S(1)}) custom-call(s32[9]{0:T(128)S(1)} %copy-done.4, f32[3,32,128]{2,1,0:T(8,128)S(1)} %copy-done.5, f32[32,128]{1,0:T(8,128)S(1)} %broadcast_in_dim.3.refs_2_, bf16[1600,2048]{1,0:T(8,128)(2,1)S(1)} %bitcast.20, ...), custom_call_target="tpu_custom_call" | custom-call | flops 3355443200 | bytes 14155776 | tf_op jit(solution)/shard_map/pallas_call | solution.py:174
  111.1 0.2 collective-permute-done.6.refs_6_
  111.3 4.7 %shard_map.140 = (f32[3,32,128]{2,1,0:T(8,128)S(1)}, f32[32,128]{1,0:T(8,128)S(1)}) custom-call(s32[9]{0:T(128)S(1)} %copy-done.4, f32[3,32,128]{2,1,0:T(8,128)S(1)} %get-tuple-element.26.refs_1_, f32[32,128]{1,0:T(8,128)S(1)} %get-tuple-element.27.refs_2_, bf16[1600,2048]{1,0:T(8,128)(2,1)S(1)} %bitcast.21, ...), custom_call_target="tpu_custom_call" | custom-call | flops 3355443200 | bytes 14155776 | tf_op jit(solution)/shard_map/pallas_call | solution.py:174
  116.1 4.6 %shard_map.141 = (f32[3,32,128]{2,1,0:T(8,128)S(1)}, f32[32,128]{1,0:T(8,128)S(1)}) custom-call(s32[9]{0:T(128)S(1)} %copy-done.4, f32[3,32,128]{2,1,0:T(8,128)S(1)} %get-tuple-element.29.refs_1_, f32[32,128]{1,0:T(8,128)S(1)} %get-tuple-element.30.refs_2_, bf16[1600,2048]{1,0:T(8,128)(2,1)S(1)} %bitcast.22, ...), custom_call_target="tpu_custom_call" | custom-call | flops 3355443200 | bytes 14155776 | tf_op jit(solution)/shard_map/pallas_call | solution.py:174
  120.7 2.5 %collective-permute-done.9.refs_6_ = bf16[136,2048]{1,0:T(8,128)(2,1)S(1)} collective-permute-done((bf16[136,2048]{1,0:T(8,128)(2,1)S(1)}, bf16[136,2048]{1,0:T(8,128)(2,1)S(1)}, u32[]{:S(2)}, u32[]{:S(2)}) %collective-permute-start.9) | collective-permute-done | bytes 557088 | tf_op jit(solution)/shard_map/ppermute | solution.py:469
  123.3 4.7 %shard_map.142 = (f32[3,32,128]{2,1,0:T(8,128)S(1)}, f32[32,128]{1,0:T(8,128)S(1)}) custom-call(s32[9]{0:T(128)S(1)} %copy-done.4, f32[3,32,128]{2,1,0:T(8,128)S(1)} %get-tuple-element.31.refs_1_, f32[32,128]{1,0:T(8,128)S(1)} %get-tuple-element.32.refs_2_, bf16[1600,2048]{1,0:T(8,128)(2,1)S(1)} %bitcast.23, ...), custom_call_target="tpu_custom_call" | custom-call | flops 3355443200 | bytes 14155776 | tf_op jit(solution)/shard_map/pallas_call | solution.py:174
  128.0 4.9 %shard_map.143 = (f32[3,32,128]{2,1,0:T(8,128)S(1)}, f32[32,128]{1,0:T(8,128)S(1)}) custom-call(s32[9]{0:T(128)S(1)} %copy-done.4, f32[3,32,128]{2,1,0:T(8,128)S(1)} %get-tuple-element.33.refs_1_, f32[32,128]{1,0:T(8,128)S(1)} %get-tuple-element.34.refs_2_, bf16[1600,2048]{1,0:T(8,128)(2,1)S(1)} %bitcast.24, ...), custom_call_target="tpu_custom_call" | custom-call | flops 3355443200 | bytes 14155776 | tf_op jit(solution)/shard_map/pallas_call | solution.py:174
  132.9 2.3 %collective-permute-done.12.refs_6_ = bf16[136,2048]{1,0:T(8,128)(2,1)S(1)} collective-permute-done((bf16[136,2048]{1,0:T(8,128)(2,1)S(1)}, bf16[136,2048]{1,0:T(8,128)(2,1)S(1)}, u32[]{:S(2)}, u32[]{:S(2)}) %collective-permute-start.12) | collective-permute-done | bytes 557088 | tf_op jit(solution)/shard_map/ppermute | solution.py:469
  135.2 4.8 %shard_map.144 = (f32[3,32,128]{2,1,0:T(8,128)S(1)}, f32[32,128]{1,0:T(8,128)S(1)}) custom-call(s32[9]{0:T(128)S(1)} %copy-done.4, f32[3,32,128]{2,1,0:T(8,128)S(1)} %get-tuple-element.35.refs_1_, f32[32,128]{1,0:T(8,128)S(1)} %get-tuple-element.36.refs_2_, bf16[1600,2048]{1,0:T(8,128)(2,1)S(1)} %bitcast.25, ...), custom_call_target="tpu_custom_call" | custom-call | flops 3355443200 | bytes 14155776 | tf_op jit(solution)/shard_map/pallas_call | solution.py:174
  140.0 4.6 %shard_map.145 = (f32[3,32,128]{2,1,0:T(8,128)S(1)}, f32[32,128]{1,0:T(8,128)S(1)}) custom-call(s32[9]{0:T(128)S(1)} %copy-done.4, f32[3,32,128]{2,1,0:T(8,128)S(1)} %get-tuple-element.37.refs_1_, f32[32,128]{1,0:T(8,128)S(1)} %get-tuple-element.38.refs_2_, bf16[1600,2048]{1,0:T(8,128)(2,1)S(1)} %bitcast.26, ...), custom_call_target="tpu_custom_call" | custom-call | flops 3355443200 | bytes 14155776 | tf_op jit(solution)/shard_map/pallas_call | solution.py:174
  144.6 4.7 %shard_map.146 = (f32[3,32,128]{2,1,0:T(8,128)S(1)}, f32[32,128]{1,0:T(8,128)}) custom-call(s32[9]{0:T(128)S(1)} %copy-done.4, f32[3,32,128]{2,1,0:T(8,128)S(1)} %get-tuple-element.39.refs_1_, f32[32,128]{1,0:T(8,128)S(1)} %get-tuple-element.40.refs_2_, bf16[1600,2048]{1,0:T(8,128)(2,1)S(1)} %bitcast.27, bf16[1600,2048]{1,0:T(8,128)(2,1)S(1)} %get-tuple-element.28.refs_4_, ...), custom_call_target="tpu_custom_call" | custom-call | flops 3355443200 | bytes 14155776 | tf_op jit(solution)/shard_map/pallas_call | solution.py:174
  149.3 0.1 collective-permute-start.17
  149.4 1.2 collective-permute-done.17
  150.7 1.4 collective-permute-start.18
  152.1 1.6 collective-permute-start.19
  153.7 0.5 collective-permute-start.20
  154.2 1.3 collective-permute-done.18
  155.5 0.5 collective-permute-done.19
  156.0 1.6 collective-permute-done.20
  157.7 1.1 collective-permute-start.21
  158.8 3.0 %collective-permute-start.22 = (f32[2,32,128]{2,1,0:T(8,128)S(1)}, f32[2,32,128]{2,1,0:T(8,128)S(1)}, u32[]{:S(2)}, u32[]{:S(2)}) collective-permute-start(f32[2,32,128]{2,1,0:T(8,128)S(1)} %pad_maximum_fusion.1.own), channel_id=1, source_target_pairs={{0,16},{1,17},{2,18},{3,19},{4,20},{5,21},{6,22},{7,23},{8,24},{9,... | collective-permute-start | bytes 98312 | tf_op jit(solution)/shard_map/ppermute | solution.py:619
  161.8 0.4 collective-permute-start.23
  162.1 1.5 collective-permute-done.22.far_low
  163.7 3.8 %collective-permute-done.23.far_high = f32[2,32,128]{2,1,0:T(8,128)S(1)} collective-permute-done((f32[2,32,128]{2,1,0:T(8,128)S(1)}, f32[2,32,128]{2,1,0:T(8,128)S(1)}, u32[]{:S(2)}, u32[]{:S(2)}) %collective-permute-start.23) | collective-permute-done | bytes 32800 | tf_op jit(solution)/shard_map/ppermute | solution.py:619
  167.5 1.2 last.1
  (30 shorter events, 0.1 us)
Async XLA Ops:
  0.6 25.1 %copy-start = (bf16[2,128,2048]{2,1,0:T(8,128)(2,1)S(1)}, bf16[2,128,2048]{2,1,0:T(8,128)(2,1)}, u32[]{:S(2)}) copy-start(bf16[2,128,2048]{2,1,0:T(8,128)(2,1)} %hidden.5) | copy-start | bytes 3145732
  0.6 25.1 %copy-start.6 = (f32[2048]{0:T(1024)S(1)}, f32[2048]{0:T(1024)}, u32[]{:S(2)}) copy-start(f32[2048]{0:T(1024)} %param.20) | copy-start | bytes 24580
  0.7 28.5 %copy-start.7 = (f32[2048]{0:T(1024)S(1)}, f32[2048]{0:T(1024)}, u32[]{:S(2)}) copy-start(f32[2048]{0:T(1024)} %param.23) | copy-start | bytes 24580
  0.7 103.5 %collective-permute-start = (bf16[1600,2048]{1,0:T(8,128)(2,1)}, bf16[1600,2048]{1,0:T(8,128)(2,1)}, u32[]{:S(2)}, u32[]{:S(2)}) collective-permute-start(bf16[1600,2048]{1,0:T(8,128)(2,1)} %bitcast.17), channel_id=1, source_target_pairs={{0,1},{1,0},{2,3},{3,2},{4,5},{5,4},{6,7},{7,6},{8,9},{9,8},{10,11... | collective-permute-start | bytes 19660808 | tf_op jit(solution)/shard_map/ppermute | solution.py:469
  2.1 5.9 %collective-permute-start.1 = (bf16[2,1,2048]{2,1,0:T(2,128)(2,1)S(1)}, bf16[2,1,2048]{2,1,0:T(2,128)(2,1)S(1)}, u32[]{:S(2)}, u32[]{:S(2)}) collective-permute-start(bf16[2,1,2048]{2,1,0:T(2,128)(2,1)S(1)} %slice.49), channel_id=1, source_target_pairs={{0,4},{4,8},{8,12},{12,16},{16,20},{20,24},{24,28},{1,5},{5,9},{9,... | collective-permute-start | bytes 24584 | tf_op jit(solution)/shard_map/ppermute | solution.py:477
  8.0 0.6 copy-start.8
  8.6 96.8 %slice-start = ((s8[6553600]{0:T(1024)(128)(4,1)}), s8[2359296]{0:T(1024)(128)(4,1)S(1)}, s32[]{:S(2)}) async-start(s8[6553600]{0:T(1024)(128)(4,1)} %bitcast.18), calls=%async_computation | async-start | bytes 4718592
  8.6 96.8 %copy-start.5 = (f32[3,32,128]{2,1,0:T(8,128)S(1)}, f32[3,32,128]{2,1,0:T(8,128)}, u32[]{:S(2)}) copy-start(f32[3,32,128]{2,1,0:T(8,128)} %constant.31.clone.1.refs_1_) | copy-start | bytes 147460
  13.6 8.2 %collective-permute-start.3 = (bf16[256,512]{1,0:T(8,128)(2,1)}, bf16[256,512]{1,0:T(8,128)(2,1)}, u32[]{:S(2)}, u32[]{:S(2)}) collective-permute-start(bf16[256,512]{1,0:T(8,128)(2,1)} %mix.1.value), channel_id=1, source_target_pairs={{0,2},{1,3},{2,0},{3,1},{4,6},{5,7},{6,4},{7,5},{8,10},{9,11},{10,... | collective-permute-start | bytes 786440 | tf_op jit(solution)/shard_map/ppermute | solution.py:469
  15.2 14.0 %collective-permute-start.2 = (bf16[256,512]{1,0:T(8,128)(2,1)}, bf16[256,512]{1,0:T(8,128)(2,1)}, u32[]{:S(2)}, u32[]{:S(2)}) collective-permute-start(bf16[256,512]{1,0:T(8,128)(2,1)} %mix.1.value), channel_id=1, source_target_pairs={{0,1},{1,0},{2,3},{3,2},{4,5},{5,4},{6,7},{7,6},{8,9},{9,8},{10,11... | collective-permute-start | bytes 786440 | tf_op jit(solution)/shard_map/ppermute | solution.py:469
  21.8 7.4 %collective-permute-start.4 = (bf16[256,512]{1,0:T(8,128)(2,1)}, bf16[256,512]{1,0:T(8,128)(2,1)}, u32[]{:S(2)}, u32[]{:S(2)}) collective-permute-start(bf16[256,512]{1,0:T(8,128)(2,1)} %collective-permute-done.3.above), channel_id=1, source_target_pairs={{0,1},{1,0},{2,3},{3,2},{4,5},{5,4},{6,7},{7,6},{8,9},{9,8},{10,11... | collective-permute-start | bytes 786440 | tf_op jit(solution)/shard_map/ppermute | solution.py:469
  22.4 83.0 %copy-start.4 = (s32[9]{0:T(128)S(1)}, s32[9]{0:T(128)}, u32[]{:S(2)}) copy-start(s32[9]{0:T(128)} %stack.49.scalars.refs_0_) | copy-start | bytes 112
  22.4 83.0 %slice-start.1 = ((s8[6553600]{0:T(1024)(128)(4,1)}), s8[4194304]{0:T(1024)(128)(4,1)S(1)}, s32[]{:S(2)}) async-start(s8[6553600]{0:T(1024)(128)(4,1)} %bitcast.18), calls=%async_computation.1 | async-start | bytes 8388608
  25.7 1.1 copy-start.1
  26.8 0.9 copy-start.2
  27.7 0.6 copy-start.3
  30.8 15.8 %collective-permute-start.7 = (bf16[256,2048]{1,0:T(8,128)(2,1)S(1)}, bf16[256,2048]{1,0:T(8,128)(2,1)S(1)}, u32[]{:S(2)}, u32[]{:S(2)}) collective-permute-start(bf16[256,2048]{1,0:T(8,128)(2,1)S(1)} %arrange.1.refs_6_), channel_id=1, source_target_pairs={{0,4},{1,9},{2,6},{3,11},{4,12},{5,1},{6,14},{7,3},{8,0},{9,17},{1... | collective-permute-start | bytes 3145736 | tf_op jit(solution)/shard_map/ppermute | solution.py:514
  46.7 21.8 %collective-permute-start.10 = (bf16[256,2048]{1,0:T(8,128)(2,1)S(1)}, bf16[256,2048]{1,0:T(8,128)(2,1)S(1)}, u32[]{:S(2)}, u32[]{:S(2)}) collective-permute-start(bf16[256,2048]{1,0:T(8,128)(2,1)S(1)} %collective-permute-done.7.refs_5_), channel_id=1, source_target_pairs={{0,4},{1,9},{2,6},{3,11},{4,12},{5,1},{6,14},{7,3},{8,0},{9,17},{1... | collective-permute-start | bytes 3145736 | tf_op jit(solution)/shard_map/ppermute | solution.py:514
  47.7 19.7 %collective-permute-start.5 = (bf16[136,2048]{1,0:T(8,128)(2,1)S(1)}, bf16[136,2048]{1,0:T(8,128)(2,1)S(1)}, u32[]{:S(2)}, u32[]{:S(2)}) collective-permute-start(bf16[136,2048]{1,0:T(8,128)(2,1)S(1)} %copy-done.1), channel_id=1, source_target_pairs={{0,4},{1,9},{2,6},{3,11},{4,12},{5,1},{6,14},{7,3},{8,0},{9,17},{1... | collective-permute-start | bytes 1671176 | tf_op jit(solution)/shard_map/ppermute | solution.py:514
  67.4 9.5 %collective-permute-start.8 = (bf16[136,2048]{1,0:T(8,128)(2,1)S(1)}, bf16[136,2048]{1,0:T(8,128)(2,1)S(1)}, u32[]{:S(2)}, u32[]{:S(2)}) collective-permute-start(bf16[136,2048]{1,0:T(8,128)(2,1)S(1)} %collective-permute-done.5.refs_5_.refs_6_), channel_id=1, source_target_pairs={{0,4},{1,9},{2,6},{3,11},{4,12},{5,1},{6,14},{7,3},{8,0},{9,17},{1... | collective-permute-start | bytes 1671176 | tf_op jit(solution)/shard_map/ppermute | solution.py:514
  68.5 34.6 %collective-permute-start.13 = (bf16[256,2048]{1,0:T(8,128)(2,1)S(1)}, bf16[256,2048]{1,0:T(8,128)(2,1)S(1)}, u32[]{:S(2)}, u32[]{:S(2)}) collective-permute-start(bf16[256,2048]{1,0:T(8,128)(2,1)S(1)} %collective-permute-done.10.refs_5_), channel_id=1, source_target_pairs={{0,4},{1,9},{2,6},{3,11},{4,12},{5,1},{6,14},{7,3},{8,0},{9,17},{1... | collective-permute-start | bytes 3145736 | tf_op jit(solution)/shard_map/ppermute | solution.py:514
  77.0 17.2 %collective-permute-start.11 = (bf16[136,2048]{1,0:T(8,128)(2,1)S(1)}, bf16[136,2048]{1,0:T(8,128)(2,1)S(1)}, u32[]{:S(2)}, u32[]{:S(2)}) collective-permute-start(bf16[136,2048]{1,0:T(8,128)(2,1)S(1)} %collective-permute-done.8.refs_5_.refs_6_), channel_id=1, source_target_pairs={{0,4},{1,9},{2,6},{3,11},{4,12},{5,1},{6,14},{7,3},{8,0},{9,17},{1... | collective-permute-start | bytes 1671176 | tf_op jit(solution)/shard_map/ppermute | solution.py:514
  94.7 6.8 %collective-permute-start.14 = (bf16[72,2048]{1,0:T(8,128)(2,1)S(1)}, bf16[72,2048]{1,0:T(8,128)(2,1)S(1)}, u32[]{:S(2)}, u32[]{:S(2)}) collective-permute-start(bf16[72,2048]{1,0:T(8,128)(2,1)S(1)} %half.2), channel_id=1, source_target_pairs={{0,4},{1,9},{2,6},{3,11},{4,12},{5,1},{6,14},{7,3},{8,0},{9,17},{1... | collective-permute-start | bytes 884744 | tf_op jit(solution)/shard_map/ppermute | solution.py:514
  95.8 15.5 %collective-permute-start.6 = (bf16[136,2048]{1,0:T(8,128)(2,1)S(1)}, bf16[136,2048]{1,0:T(8,128)(2,1)S(1)}, u32[]{:S(2)}, u32[]{:S(2)}) collective-permute-start(bf16[136,2048]{1,0:T(8,128)(2,1)S(1)} %collective-permute-done.5.refs_5_.refs_6_), channel_id=1, source_target_pairs={{0,2},{1,3},{2,0},{3,1},{4,6},{5,7},{6,4},{7,5},{8,10},{9,11},{10,... | collective-permute-start | bytes 1671176 | tf_op jit(solution)/shard_map/ppermute | solution.py:469
  97.3 25.9 %collective-permute-start.9 = (bf16[136,2048]{1,0:T(8,128)(2,1)S(1)}, bf16[136,2048]{1,0:T(8,128)(2,1)S(1)}, u32[]{:S(2)}, u32[]{:S(2)}) collective-permute-start(bf16[136,2048]{1,0:T(8,128)(2,1)S(1)} %collective-permute-done.8.refs_5_.refs_6_), channel_id=1, source_target_pairs={{0,2},{1,3},{2,0},{3,1},{4,6},{5,7},{6,4},{7,5},{8,10},{9,11},{10,... | collective-permute-start | bytes 1671176 | tf_op jit(solution)/shard_map/ppermute | solution.py:469
  101.5 33.7 %collective-permute-start.12 = (bf16[136,2048]{1,0:T(8,128)(2,1)S(1)}, bf16[136,2048]{1,0:T(8,128)(2,1)S(1)}, u32[]{:S(2)}, u32[]{:S(2)}) collective-permute-start(bf16[136,2048]{1,0:T(8,128)(2,1)S(1)} %collective-permute-done.11.refs_5_.refs_6_.block), channel_id=1, source_target_pairs={{0,2},{1,3},{2,0},{3,1},{4,6},{5,7},{6,4},{7,5},{8,10},{9,11},{10,... | collective-permute-start | bytes 1671176 | tf_op jit(solution)/shard_map/ppermute | solution.py:469
  103.0 41.6 %collective-permute-start.15 = (bf16[72,2048]{1,0:T(8,128)(2,1)S(1)}, bf16[72,2048]{1,0:T(8,128)(2,1)S(1)}, u32[]{:S(2)}, u32[]{:S(2)}) collective-permute-start(bf16[72,2048]{1,0:T(8,128)(2,1)S(1)} %collective-permute-done.14.refs_5_), channel_id=1, source_target_pairs={{0,2},{1,3},{2,0},{3,1},{4,6},{5,7},{6,4},{7,5},{8,10},{9,11},{10,... | collective-permute-start | bytes 884744 | tf_op jit(solution)/shard_map/ppermute | solution.py:469
  104.1 40.5 %collective-permute-start.16 = (bf16[128,2048]{1,0:T(8,128)(2,1)S(1)}, bf16[128,2048]{1,0:T(8,128)(2,1)S(1)}, u32[]{:S(2)}, u32[]{:S(2)}) collective-permute-start(bf16[128,2048]{1,0:T(8,128)(2,1)S(1)} %half.3), channel_id=1, source_target_pairs={{0,4},{1,9},{2,6},{3,11},{4,12},{5,1},{6,14},{7,3},{8,0},{9,17},{1... | collective-permute-start | bytes 1572872 | tf_op jit(solution)/shard_map/ppermute | solution.py:514
  149.3 1.3 collective-permute-start.17
  150.7 4.9 %collective-permute-start.18 = (f32[2,32,128]{2,1,0:T(8,128)S(1)}, f32[2,32,128]{2,1,0:T(8,128)S(1)}, u32[]{:S(2)}, u32[]{:S(2)}) collective-permute-start(f32[2,32,128]{2,1,0:T(8,128)S(1)} %pad_maximum_fusion), channel_id=1, source_target_pairs={{0,6},{1,7},{2,4},{3,5},{4,2},{5,3},{6,0},{7,1},{8,14},{9,15},{10,... | collective-permute-start | bytes 98312 | tf_op jit(solution)/shard_map/ppermute | solution.py:619
  152.1 3.9 %collective-permute-start.19 = (f32[2,32,128]{2,1,0:T(8,128)S(1)}, f32[2,32,128]{2,1,0:T(8,128)S(1)}, u32[]{:S(2)}, u32[]{:S(2)}) collective-permute-start(f32[2,32,128]{2,1,0:T(8,128)S(1)} %pad_maximum_fusion), channel_id=1, source_target_pairs={{0,4},{1,5},{2,6},{3,7},{4,0},{5,1},{6,2},{7,3},{8,12},{9,13},{10,... | collective-permute-start | bytes 98312 | tf_op jit(solution)/shard_map/ppermute | solution.py:619
  153.7 3.9 %collective-permute-start.20 = (f32[2,32,128]{2,1,0:T(8,128)S(1)}, f32[2,32,128]{2,1,0:T(8,128)S(1)}, u32[]{:S(2)}, u32[]{:S(2)}) collective-permute-start(f32[2,32,128]{2,1,0:T(8,128)S(1)} %pad_maximum_fusion), channel_id=1, source_target_pairs={{0,2},{1,3},{2,0},{3,1},{4,6},{5,7},{6,4},{7,5},{8,10},{9,11},{10,... | collective-permute-start | bytes 98312 | tf_op jit(solution)/shard_map/ppermute | solution.py:619
  157.7 4.5 %collective-permute-start.21 = (f32[2,32,128]{2,1,0:T(8,128)S(1)}, f32[2,32,128]{2,1,0:T(8,128)S(1)}, u32[]{:S(2)}, u32[]{:S(2)}) collective-permute-start(f32[2,32,128]{2,1,0:T(8,128)S(1)} %pad_maximum_fusion.1.own), channel_id=1, source_target_pairs={{0,8},{1,9},{2,10},{3,11},{4,12},{5,13},{6,14},{7,15},{8,0},{9,1},... | collective-permute-start | bytes 98312 | tf_op jit(solution)/shard_map/ppermute | solution.py:619
  158.8 4.9 %collective-permute-start.22 = (f32[2,32,128]{2,1,0:T(8,128)S(1)}, f32[2,32,128]{2,1,0:T(8,128)S(1)}, u32[]{:S(2)}, u32[]{:S(2)}) collective-permute-start(f32[2,32,128]{2,1,0:T(8,128)S(1)} %pad_maximum_fusion.1.own), channel_id=1, source_target_pairs={{0,16},{1,17},{2,18},{3,19},{4,20},{5,21},{6,22},{7,23},{8,24},{9,... | collective-permute-start | bytes 98312 | tf_op jit(solution)/shard_map/ppermute | solution.py:619
  161.8 5.7 %collective-permute-start.23 = (f32[2,32,128]{2,1,0:T(8,128)S(1)}, f32[2,32,128]{2,1,0:T(8,128)S(1)}, u32[]{:S(2)}, u32[]{:S(2)}) collective-permute-start(f32[2,32,128]{2,1,0:T(8,128)S(1)} %pad_maximum_fusion.1.own), channel_id=1, source_target_pairs={{0,24},{1,25},{2,26},{3,27},{4,28},{5,29},{6,30},{7,31},{8,16},{9,... | collective-permute-start | bytes 98312 | tf_op jit(solution)/shard_map/ppermute | solution.py:619
